TPU v7x, 32 devices: a whole 2x2x4 slice. The times are simulated.
32 devices in a mesh: dp: 2 (over x), fsdp: 4 (over z), tp: 4 (over y, core).
Axes of the slice: x: 2, y: 2, z: 4, core: 2. Of those that a mesh axis runs over, the one named last changes fastest.
Arguments:
- hidden: bfloat16 [16384, 768], P(('dp', 'fsdp', 'tp')), parts along dimension 0
- w_head: bfloat16 [768, 50304], P('fsdp', 'tp')
- labels: int32 [16384], P(('dp', 'fsdp', 'tp')), parts along dimension 0
Outputs:
- output 1: float32 [2], P('dp'), parts along dimension 0
- output 2: bfloat16 [16384, 768], P(('dp', 'fsdp', 'tp')), parts along dimension 0
- output 3: bfloat16 [1536, 50304], P(('dp', 'fsdp'), 'tp'), parts along dimension 0
There are 2 independent parts. A program takes and returns all parts, laid end to end along the dimension named above; an argument that names none is the same for every part.
All inputs are finite; a program needn't handle non-finite values.
Results may differ from a plain program's by a relative error of at most 0.001.
Values are sent between devices in bfloat16 or wider.
A program may use at most 1 GiB of HBM per device.

v0:
```python
import jax
import jax.numpy as jnp
from jax import lax
from jax.sharding import PartitionSpec as P


def solution(mesh):
    fsdp_size = mesh.shape["fsdp"]
    tp_size = mesh.shape["tp"]
    token_spec = P(("dp", "fsdp", "tp"), None)
    label_spec = P(("dp", "fsdp", "tp"))

    def local_step(hidden, w_head, labels):
        rows_dev = hidden.shape[0]
        vocab_dev = w_head.shape[1]
        inv_tokens = 1.0 / (rows_dev * tp_size * fsdp_size)
        w_full = lax.all_gather(w_head, "fsdp", axis=0, tiled=True)
        x_full = lax.all_gather(hidden, "tp", axis=0, tiled=True)
        lab_full = lax.all_gather(labels, "tp", axis=0, tiled=True)
        logits = jnp.dot(x_full, w_full, preferred_element_type=jnp.float32)
        row_max = lax.pmax(jnp.max(logits, axis=1), "tp")
        exp_rows = jnp.exp(logits - row_max[:, None])
        local_ids = lab_full - lax.axis_index("tp") * vocab_dev
        onehot = local_ids[:, None] == jnp.arange(vocab_dev, dtype=jnp.int32)[None, :]
        local_stats = jnp.stack([jnp.sum(exp_rows, axis=1), jnp.sum(jnp.where(onehot, logits, 0.0), axis=1)])
        stat_sums = lax.psum(local_stats, "tp")
        row_sum = stat_sums[0]
        target = stat_sums[1]
        tok_loss = row_max + jnp.log(row_sum) - target
        mean_loss = lax.psum(jnp.sum(tok_loss), "fsdp") * inv_tokens
        prob_rows = exp_rows / row_sum[:, None]
        grad_logits = (jnp.where(onehot, prob_rows - 1.0, prob_rows) * inv_tokens).astype(jnp.bfloat16)
        d_x_part = jnp.einsum("tv,hv->th", grad_logits, w_full, preferred_element_type=jnp.float32)
        d_hidden = lax.psum_scatter(d_x_part, "tp", scatter_dimension=0, tiled=True).astype(jnp.bfloat16)
        d_w_part = jnp.einsum("th,tv->hv", x_full, grad_logits, preferred_element_type=jnp.float32)
        d_w_head = lax.psum_scatter(d_w_part, "fsdp", scatter_dimension=0, tiled=True).astype(jnp.bfloat16)
        return mean_loss.reshape(1), d_hidden, d_w_head

    return jax.shard_map(
        local_step,
        mesh=mesh,
        in_specs=(token_spec, P("fsdp", "tp"), label_spec),
        out_specs=(P("dp"), token_spec, P(("dp", "fsdp"), "tp")),
        check_vma=False,
    )
```

profile of v0, /device:TPU:0, one launch (start us, length us, event | category | flops | bytes accessed | tf_op | source)
XLA Modules:
  0.0 1325.5 jit_solution(5079852258094908371)
XLA Ops:
  7.2 0.0 all-gather.4.cloned.1.call-start
  7.2 0.7 all-gather.4.cloned.1.call-update
  7.9 0.0 all-gather.6.cloned.1.call-start
  7.9 0.7 all-gather.6.cloned.1.call-update
  8.6 0.0 reduce-scatter.5.cloned.1.call-start
  8.7 6.2 all-gather
  14.9 25.7 %all-gather.4.cloned.1.call-done = bf16[2048,768]{1,0:T(8,128)(2,1)} async-done(((bf16[512,768]{1,0:T(8,128)(2,1)}), bf16[2048,768]{1,0:T(8,128)(2,1)}) %all-gather.4.cloned.1.call-update) | async-done | bytes 3145744 | tf_op jit(solution)/shard_map/all_gather | solution.py:18
  40.6 334.6 %all-gather.6.cloned.1.call-done = bf16[768,12576]{1,0:T(8,128)(2,1)} async-done(((bf16[192,12576]{1,0:T(8,128)(2,1)}), bf16[768,12576]{1,0:T(8,128)(2,1)}) %all-gather.6.cloned.1.call-update) | async-done | bytes 19316752 | tf_op jit(solution)/shard_map/all_gather | solution.py:17
  375.1 51.2 %fusion.4 = (f32[2048]{0:T(1024)S(1)}, f32[2048,12576]{0,1:T(8,128)}) fusion(bf16[2048,768]{1,0:T(8,128)(2,1)} %all-gather.4.cloned.1.call-done, bf16[768,12576]{1,0:T(8,128)(2,1)} %all-gather.6.cloned.1.call-done), kind=kOutput, calls=%fused_computation.12 | convolution fusion | flops 39586430976 | bytes 125493248 | tf_op jit(solution)/shard_map/dot_general | solution.py:20
  426.3 6.3 pmax.7
  432.6 32.1 %fusion.2 = (f32[2048]{0:T(1024)S(1)}, f32[2048]{0:T(1024)S(1)}) fusion(f32[2048,12576]{0,1:T(8,128)} %get-tuple-element.14, f32[2048]{0:T(1024)S(1)} %pmax.7, s32[2048]{0:T(1024)S(1)} %bitcast.16), kind=kLoop, calls=%fused_computation.6 | loop fusion | flops 128774144 | bytes 103055360 | tf_op jit(solution)/shard_map/reduce_sum | solution.py:25
  464.8 10.4 psum.14
  475.1 0.6 fusion.3
  475.8 50.2 %fusion.1 = bf16[2048,12576]{0,1:T(8,128)(2,1)} fusion(f32[2048,12576]{0,1:T(8,128)} %get-tuple-element.14, f32[2048]{0:T(1024)S(1)} %bitcast.18, s32[2048]{0:T(1024)S(1)} %bitcast.17, f32[2048]{0:T(1024)S(1)} %pmax.7), kind=kLoop, calls=%fused_computation.2 | loop fusion | flops 180289536 | bytes 154558464 | tf_op jit(solution)/shard_map/convert_element_type | solution.py:32
  526.0 51.5 %fusion.5 = f32[2048,768]{1,0:T(8,128)} fusion(bf16[2048,12576]{0,1:T(8,128)(2,1)} %fusion.1, bf16[768,12576]{1,0:T(8,128)(2,1)} %all-gather.6.cloned.1.call-done), kind=kOutput, calls=%fused_computation.13 | convolution fusion | flops 39560675328 | bytes 77119488 | tf_op jit(solution)/shard_map/tv,hv->th/dot_general | solution.py:33
  577.6 0.3 reduce-scatter.7.cloned.1.call-start
  577.9 47.9 %convolution_bitcast_fusion = f32[768,12576]{0,1:T(8,128)} fusion(bf16[2048,12576]{0,1:T(8,128)(2,1)} %fusion.1, bf16[2048,768]{1,0:T(8,128)(2,1)S(1)} %copy-done.5), kind=kOutput, calls=%fused_computation.7 | convolution fusion | flops 39560675328 | bytes 93290496 | tf_op jit(solution)/shard_map/th,tv->hv/dot_general | solution.py:35
  625.7 38.6 %copy.8 = f32[768,12576]{1,0:T(8,128)} copy(f32[768,12576]{0,1:T(8,128)} %convolution_bitcast_fusion) | data formatting | bytes 77266944
  664.4 0.6 subtract_reduce_fusion
  665.0 10.9 psum.15
  676.5 2.4 convert_element_type.10
  678.9 621.3 %reduce-scatter.7.cloned.1.call-done = f32[192,12576]{1,0:T(8,128)} async-done(((f32[768,12576]{1,0:T(8,128)}), f32[192,12576]{1,0:T(8,128)}) %reduce-scatter.7.cloned.1.call-update) | async-done | bytes 9658384
  1300.2 9.5 copy.9
  1309.7 8.2 copy.7
  (17 shorter events, 0.1 us)
Async XLA Ops:
  7.2 33.4 %all-gather.4.cloned.1.call-start = ((), (), s32[]{:S(2)}) async-start(), calls=%async_computation.2 | async-start | bytes 3932160 | tf_op jit(solution)/shard_map/all_gather | solution.py:18
  7.9 367.2 %all-gather.6.cloned.1.call-start = ((), (), s32[]{:S(2)}) async-start(), calls=%async_computation.3 | async-start | bytes 24330240 | tf_op jit(solution)/shard_map/all_gather | solution.py:17
  8.6 667.9 %reduce-scatter.5.cloned.1.call-start = ((), (), s32[]{:S(2)}) async-start(), calls=%async_computation.4 | async-start | bytes 7864320 | tf_op jit(solution)/shard_map/reduce_scatter | solution.py:34
  432.6 43.2 %copy-start = (f32[2048]{0:T(1024)}, f32[2048]{0:T(1024)S(1)}, u32[]{:S(2)}) copy-start(f32[2048]{0:T(1024)S(1)} %pmax.7) | copy-start | bytes 24580
  475.8 50.2 %copy-start.2 = (f32[1,2048]{1,0:T(1,128)}, f32[1,2048]{1,0:T(1,128)S(1)}, u32[]{:S(2)}) copy-start(f32[1,2048]{1,0:T(1,128)S(1)} %get-tuple-element.11) | copy-start | bytes 24580
  526.0 51.9 %copy-start.5 = (bf16[2048,768]{1,0:T(8,128)(2,1)S(1)}, bf16[2048,768]{1,0:T(8,128)(2,1)}, u32[]{:S(2)}) copy-start(bf16[2048,768]{1,0:T(8,128)(2,1)} %all-gather.4.cloned.1.call-done) | copy-start | bytes 9437188
  577.6 722.6 %reduce-scatter.7.cloned.1.call-start = ((), (), s32[]{:S(2)}) async-start(), calls=%async_computation.5 | async-start | bytes 48660480
  625.7 38.6 %copy-start.1 = (f32[2048]{0:T(1024)S(1)}, f32[2048]{0:T(1024)}, u32[]{:S(2)}) copy-start(f32[2048]{0:T(1024)} %copy-done) | copy-start | bytes 24580
  625.7 38.6 %copy-start.3 = (f32[1,2048]{1,0:T(1,128)S(1)}, f32[1,2048]{1,0:T(1,128)}, u32[]{:S(2)}) copy-start(f32[1,2048]{1,0:T(1,128)} %copy-done.2) | copy-start | bytes 24580
  625.7 38.6 %copy-start.4 = (f32[1,2048]{1,0:T(1,128)S(1)}, f32[1,2048]{1,0:T(1,128)}, u32[]{:S(2)}) copy-start(f32[1,2048]{1,0:T(1,128)} %get-tuple-element.12) | copy-start | bytes 24580
Sparse Core Ops, SparseCore 0:
  9.5 30.9 all-gather.3
  42.1 332.9 all-gather.5
  577.7 55.7 reduce-scatter.4
  664.5 635.7 reduce-scatter.6
where the time goes:
time: 1330 us
  waiting for transfers between devices  983 us (74%)
  matrix products  151 us (11%)
  other arithmetic  85.4 us (6%)
  local copies, waits for them, and re-layouts  56.9 us (4%)
  blocking collectives  33.7 us (3%)
  between operations  15.6 us (1%)
    unnamed x5, waiting for transfers between devices  623 us
    all_gather x1, waiting for transfers between devices, local_step(): w_full = lax.all_gather(w_head, 'fsdp', axis=0, tiled=True)  335 us
    unnamed x15, local copies, waits for them, and re-layouts  56.3 us
    dot_general x1, matrix products, local_step(): jnp.einsum('tv,hv->th', grad_logits, w_full, preferred_element_type=jnp.f...  51.5 us
    dot_general x1, matrix products, local_step(): logits = jnp.dot(x_full, w_full, preferred_element_type=jnp.float32)  51.2 us
    convert_element_type x1, other arithmetic, local_step(): (jnp.where(onehot, prob_rows - 1.0, prob_rows) * inv_tokens).astype(jnp.b...  50.2 us
    dot_general x1, matrix products, local_step(): jnp.einsum('th,tv->hv', x_full, grad_logits, preferred_element_type=jnp.f...  47.9 us
    reduce_sum x1, other arithmetic, local_step(): jnp.sum(exp_rows, axis=1)  32.1 us
  transfers between devices with their start and end apart: 4, of which 3 were waited for; matrix products, arithmetic and copies ran while one was open for 7% of the time, Pallas kernels for 0%

commit v1 on v0

v1 whole, which is shorter than its diff:
```python
import functools

import jax
import jax.numpy as jnp
from jax import lax
from jax.experimental import pallas as pl
from jax.experimental.pallas import tpu as pltpu
from jax.sharding import PartitionSpec as P


LANES = 128
MESH = pl.DeviceIdType.MESH
NEG = -3.0e38
VMEM_LIMIT = 60 * 1024 * 1024
CHUNKS = 4
STATS = 4


def _ceil_to(n, m):
    return -(-n // m) * m


def _rows_to_cols(ref):
    cols = [jnp.concatenate([ref[b]] * (LANES // ref.shape[1]), axis=0).T for b in range(ref.shape[0])]
    return jnp.concatenate(cols, axis=0)


def _tiles(vp):
    width = vp // 4 // 256 * 256
    edges = [0, width, 2 * width, 3 * width, vp]
    return list(zip(edges[:-1], edges[1:]))


def _logits_kernel(vp, valid_ref, x_ref, w_ref, lab_ref, z_ref, st_ref, xt_ref, m_ref, s_ref, t_ref, l_ref):
    rows, _ = x_ref.shape[1:]
    valid = valid_ref[0]
    x = x_ref[0]
    lane = lax.broadcasted_iota(jnp.int32, (rows, LANES), 1)
    l_ref[...] = _rows_to_cols(lab_ref)[:, 0:1].astype(jnp.int32) - lane
    m_ref[...] = jnp.full((rows, LANES), NEG, jnp.float32)
    s_ref[...] = jnp.zeros((rows, LANES), jnp.float32)
    t_ref[...] = jnp.zeros((rows, LANES), jnp.float32)
    step = 32

    def stats(c0, c1):
        for r in range(0, rows, step):
            sl = slice(r, r + step)
            zs = [z_ref[0, sl, k:k + LANES] for k in range(c0, c1, LANES)]
            off = l_ref[sl, :]
            t = t_ref[sl, :]
            m_old = m_ref[sl, :]
            m = m_old
            for zk, k in zip(zs, range(c0, c1, LANES)):
                t = t + jnp.where(off == k, zk, 0.0)
                m = jnp.maximum(m, zk)
            s = s_ref[sl, :] * jnp.exp(m_old - m)
            for zk in zs:
                s = s + jnp.exp(zk - m)
            m_ref[sl, :] = m
            s_ref[sl, :] = s
            t_ref[sl, :] = t

    before = None
    for c0, c1 in _tiles(vp):
        z = jnp.dot(x, w_ref[:, c0:c1], preferred_element_type=jnp.float32)
        if c1 == vp:
            edge = (vp - 2 * LANES - c0) // LANES * LANES
            z_ref[0, :, c0:c0 + edge] = z[:, :edge]
            for k in range(edge, c1 - c0, LANES):
                z_ref[0, :, c0 + k:c0 + k + LANES] = jnp.where(lane < valid - (c0 + k), z[:, k:k + LANES], NEG)
        else:
            z_ref[0, :, c0:c1] = z
        if before is not None:
            stats(*before)
        before = (c0, c1)
    xt_ref[...] = x.T
    stats(*before)
    m = m_ref[...]
    m_row = jnp.max(m, axis=1, keepdims=True)
    s_row = jnp.sum(s_ref[...] * jnp.exp(m - m_row), axis=1, keepdims=True)
    t_row = jnp.sum(t_ref[...], axis=1, keepdims=True)
    packed = jnp.where(lane == 0, m_row, jnp.where(lane == 1, s_row, t_row))
    st_ref[0] = packed.T[0:STATS, :]


def _grad_kernel(v0, inv_tokens, ids_ref, z_ref, w_ref, st_ref, lab_ref, *rest):
    g0_ref, g1_ref, keep_ref, send_ref = rest[-4:]
    blocks, sub, vp = z_ref.shape
    rows = blocks * sub
    st = _rows_to_cols(st_ref)
    m_row = st[:, 0:1]
    scale = st[:, 1:2] * inv_tokens
    lab_off = _rows_to_cols(lab_ref)[:, 0:1].astype(jnp.int32) - lax.broadcasted_iota(jnp.int32, (rows, LANES), 1)
    dims = (((1,), (1,)), ((), ()))

    for k in range(0, vp, LANES):
        p = jnp.exp(z_ref[:, :, k:k + LANES].reshape(rows, LANES) - m_row) * scale
        g = jnp.where(lab_off == k, p - inv_tokens, p).astype(jnp.bfloat16).reshape(blocks, sub, LANES)
        if k < v0:
            g0_ref[:, :, k:k + LANES] = g
        else:
            g1_ref[:, :, k - v0:k - v0 + LANES] = g
    total = lax.dot_general(g0_ref[...].reshape(rows, v0), w_ref[:, :v0], dims, preferred_element_type=jnp.float32)
    total = total + lax.dot_general(g1_ref[...].reshape(rows, vp - v0), w_ref[:, v0:], dims, preferred_element_type=jnp.float32)
    total = total.reshape(keep_ref.shape)
    i = pl.program_id(0)

    @pl.when(i < 2)
    def _():
        send_ref[...] = total

    @pl.when(i >= 2)
    def _():
        keep_ref[...] = total


def _dw_kernel(steps, xt_ref, g_ref, o_ref, acc_ref):
    k = pl.program_id(0)

    @pl.when(k == 0)
    def _():
        acc_ref[...] = jnp.zeros_like(acc_ref)

    g = g_ref[...].reshape(xt_ref.shape[1], g_ref.shape[2])
    acc_ref[...] += jnp.dot(xt_ref[...], g, preferred_element_type=jnp.float32)

    @pl.when(k == steps - 1)
    def _():
        o_ref[...] = acc_ref[...].astype(o_ref.dtype)


def _gather_kernel(w_ref, x_ref, l_ref, wf_ref, xf_ref, lf_ref, w_buf, x_buf, l_buf, loc,
                   w_s, w_r, wx_s, wx_r, x_s, x_r, y_s, y_r, c_s, c_r, l_s, l_r):
    n_z, n_tp = 4, 4
    n = n_z * n_tp
    dp, zi, tp = lax.axis_index("dp"), lax.axis_index("fsdp"), lax.axis_index("tp")
    w_rows = w_ref.shape[0]
    half = w_rows // 2
    vp = wf_ref.shape[1]
    mine = tp * n_z + zi

    def dev(p):
        return (dp, lax.rem(p, n_z), lax.div(p, n_z))

    peers = [dev(lax.rem(mine + o, n)) for o in range(n)]
    y_tp, c_tp = lax.rem(tp + 2, n_tp), tp + 1 - 2 * lax.rem(tp, 2)
    y_dev, c_dev, x_dev = (dp, zi, y_tp), (dp, zi, c_tp), (1 - dp, zi, tp)
    near, far, third = zi + 1 - 2 * lax.rem(zi, 2), lax.rem(zi + 2, n_z), n_z - 1 - zi
    z_owner = [zi, near, far, third]
    near_dev, far_dev = (dp, near, tp), (dp, far, tp)

    barrier = pltpu.get_barrier_semaphore()
    for d in peers[1:] + [x_dev]:
        pl.semaphore_signal(barrier, inc=1, device_id=d, device_id_type=MESH)
    pl.semaphore_wait(barrier, n)

    def remote(src, dst, s_sem, r_sem, d):
        return pltpu.make_async_remote_copy(src, dst, s_sem, r_sem, device_id=d, device_id_type=MESH)

    def w_half(owner, part):
        return wf_ref.at[pl.ds(pl.multiple_of(owner * w_rows + part * half, 8), half), :]

    def w_cols(z):
        return pl.ds(pl.multiple_of(z * vp, LANES), vp)

    sends = []

    def go(copy):
        copy.start()
        sends.append(copy)
        return copy

    load_x = pltpu.make_async_copy(x_ref, x_buf, loc.at[0])
    load_w = pltpu.make_async_copy(w_ref.at[:, w_cols(zi)], w_buf, loc.at[1])
    load_l = pltpu.make_async_copy(l_ref, l_buf, loc.at[2])
    load_x.start()
    load_w.start()
    load_l.start()
    x_in = [None] * n_z
    x_in[2] = go(remote(x_ref, xf_ref.at[mine], x_s.at[2], x_r.at[2], far_dev))
    x_in[1] = go(remote(x_ref, xf_ref.at[mine], x_s.at[1], x_r.at[1], near_dev))
    y_in = [go(remote(x_ref, xf_ref.at[mine], y_s.at[0], y_r.at[0], y_dev))]
    c_in = [go(remote(x_ref, xf_ref.at[mine], c_s.at[0], c_r.at[0], c_dev))]
    l_in = [go(remote(l_ref, lf_ref.at[mine], l_s.at[o], l_r.at[o], peers[o])) for o in range(1, n)]
    w_in = [None] * n_z
    for s in (2, 1, 3):
        src = w_ref.at[pl.ds(pl.multiple_of(dp * half, 8), half), w_cols(lax.rem(zi + s, n_z))]
        w_in[s] = go(remote(src, w_half(zi, dp), w_s.at[s], w_r.at[s], (dp, lax.rem(zi + s, n_z), tp)))
    load_x.wait()
    load_w.wait()
    load_l.wait()
    store_x = pltpu.make_async_copy(x_buf, xf_ref.at[mine], loc.at[0])
    store_w = pltpu.make_async_copy(w_buf, wf_ref.at[pl.ds(pl.multiple_of(zi * w_rows, 8), w_rows), :], loc.at[1])
    store_l = pltpu.make_async_copy(l_buf, lf_ref.at[mine], loc.at[2])
    store_x.start()
    store_w.start()
    store_l.start()
    wx_in = []
    for j in (2, 1, 3):
        x_in[j].wait_recv()
        blk = xf_ref.at[tp * n_z + z_owner[j]]
        if j == 2:
            x_in[3] = go(remote(blk, blk, x_s.at[3], x_r.at[3], near_dev))
        y_in.append(go(remote(blk, blk, y_s.at[j], y_r.at[j], y_dev)))
        c_in.append(go(remote(blk, blk, c_s.at[j], c_r.at[j], c_dev)))
        if j == 3:
            break
        w_in[j].wait_recv()
        part = w_half(lax.rem(zi + n_z - j, n_z), dp)
        wx_in.append(go(remote(part, part, wx_s.at[j], wx_r.at[j], x_dev)))
    w_in[3].wait_recv()
    part = w_half(lax.rem(zi + 1, n_z), dp)
    wx_in.append(go(remote(part, part, wx_s.at[3], wx_r.at[3], x_dev)))
    for copy, j in zip(y_in, (0, 2, 1, 3)):
        copy.wait_recv()
        blk = xf_ref.at[y_tp * n_z + z_owner[j]]
        c_in.append(go(remote(blk, blk, c_s.at[n_z + j], c_r.at[n_z + j], c_dev)))
    for copy in wx_in + c_in + l_in:
        copy.wait_recv()
    for copy in sends:
        copy.wait_send()
    store_x.wait()
    store_w.wait()
    store_l.wait()


def _gather_call(w_pad, hidden, labels, vp, n_blocks):
    w_rows = w_pad.shape[0]
    rows, hid = hidden.shape
    dma = pltpu.SemaphoreType.DMA
    return pl.pallas_call(
        _gather_kernel,
        in_specs=[pl.BlockSpec(memory_space=pl.ANY)] * 3,
        out_specs=[pl.BlockSpec(memory_space=pl.ANY)] * 3,
        out_shape=[
            jax.ShapeDtypeStruct((hid, vp), jnp.bfloat16),
            jax.ShapeDtypeStruct((n_blocks, rows, hid), jnp.bfloat16),
            jax.ShapeDtypeStruct((n_blocks,) + labels.shape, jnp.int32),
        ],
        scratch_shapes=[
            pltpu.VMEM((w_rows, vp), jnp.bfloat16),
            pltpu.VMEM((rows, hid), jnp.bfloat16),
            pltpu.VMEM(labels.shape, jnp.int32),
            dma((3,)),
        ] + [dma((4,))] * 8 + [dma((8,))] * 2 + [dma((16,))] * 2,
        compiler_params=pltpu.CompilerParams(collective_id=0, has_side_effects=True, vmem_limit_bytes=VMEM_LIMIT),
        name="gather",
    )(w_pad, hidden, labels)


def _stats_kernel(st_ref, o_ref, got, s1, r1, s2, r2):
    n, n_z = 16, 4
    dp, zi, tp = lax.axis_index("dp"), lax.axis_index("fsdp"), lax.axis_index("tp")
    me = tp * n_z + zi

    def dev(p):
        return (dp, lax.rem(p, n_z), lax.div(p, n_z))

    peers = [lax.rem(me + o, n) for o in range(n)]
    barrier = pltpu.get_barrier_semaphore()
    for o in range(1, n):
        pl.semaphore_signal(barrier, inc=1, device_id=dev(peers[o]), device_id_type=MESH)
    pl.semaphore_wait(barrier, n - 1)
    first = [
        pltpu.make_async_remote_copy(st_ref.at[peers[o]], got.at[o], s1.at[o], r1.at[o], device_id=dev(peers[o]), device_id_type=MESH)
        for o in range(1, n)
    ]
    for copy in first:
        copy.start()
    got[0] = st_ref[me]
    for copy in first:
        copy.wait_recv()
    parts = [got[o] for o in range(n)]
    m_row = parts[0][0:1]
    for p in parts[1:]:
        m_row = jnp.maximum(m_row, p[0:1])
    s_row = jnp.zeros_like(m_row)
    t_row = jnp.zeros_like(m_row)
    for p in parts:
        s_row = s_row + p[1:2] * jnp.exp(p[0:1] - m_row)
        t_row = t_row + p[2:3]
    loss = m_row + jnp.log(s_row) - t_row
    o_ref[me] = jnp.concatenate([m_row, 1.0 / s_row, loss, m_row], axis=0)
    second = [
        pltpu.make_async_remote_copy(o_ref.at[me], o_ref.at[me], s2.at[o], r2.at[o], device_id=dev(peers[o]), device_id_type=MESH)
        for o in range(1, n)
    ]
    for copy in first:
        copy.wait_send()
    for copy in second:
        copy.start()
    for copy in second:
        copy.wait()


def _stats_call(st):
    n = st.shape[0]
    vmem = pl.BlockSpec(memory_space=pltpu.VMEM)
    return pl.pallas_call(
        _stats_kernel,
        in_specs=[vmem],
        out_specs=vmem,
        out_shape=jax.ShapeDtypeStruct(st.shape, jnp.float32),
        scratch_shapes=[pltpu.VMEM(st.shape, jnp.float32)] + [pltpu.SemaphoreType.DMA((n,))] * 4,
        compiler_params=pltpu.CompilerParams(collective_id=1, has_side_effects=True),
        name="stats",
    )(st)


def _logits_call(x_all, w, lab, valid):
    n_blocks, rows, hid = x_all.shape
    vp = w.shape[1]
    tokens = n_blocks * rows
    return pl.pallas_call(
        functools.partial(_logits_kernel, vp),
        grid=(n_blocks,),
        in_specs=[
            pl.BlockSpec(memory_space=pltpu.SMEM),
            pl.BlockSpec((1, rows, hid), lambda i: (i, 0, 0)),
            pl.BlockSpec((hid, vp), lambda i: (0, 0)),
            pl.BlockSpec((1, 8, rows), lambda i: (i, 0, 0)),
        ],
        out_specs=[
            pl.BlockSpec((1, rows, vp), lambda i: (i, 0, 0)),
            pl.BlockSpec((1, STATS, rows), lambda i: (i, 0, 0)),
            pl.BlockSpec((hid, rows), lambda i: (0, i)),
        ],
        out_shape=[
            jax.ShapeDtypeStruct((n_blocks, rows, vp), jnp.float32),
            jax.ShapeDtypeStruct((n_blocks, STATS, rows), jnp.float32),
            jax.ShapeDtypeStruct((hid, tokens), jnp.bfloat16),
        ],
        scratch_shapes=[pltpu.VMEM((rows, LANES), jnp.float32)] * 3 + [pltpu.VMEM((rows, LANES), jnp.int32)],
        compiler_params=pltpu.CompilerParams(vmem_limit_bytes=VMEM_LIMIT),
        cost_estimate=pl.CostEstimate(flops=2 * tokens * hid * vp, bytes_accessed=tokens * vp * 4, transcendentals=tokens * vp),
        name="logits_stats",
    )(valid, x_all, w, lab)


def _grad_call(c, ids, z, w, st, lab, g_all, v0, sub):
    n_blocks, rows, vp = z.shape
    hid = w.shape[0]
    nb = 4
    tokens = n_blocks * rows
    extra = [] if g_all is None else list(g_all)

    def tp_of(i, ids):
        core = lax.rem(ids[0] + 1 + lax.div(i, 2), 2)
        y = lax.rem(ids[1] + lax.rem(i, 2), 2)
        return y * 2 + core

    def at(i, ids):
        return (tp_of(i, ids), c, 0)

    def at_row(i, ids):
        return (tp_of(i, ids), 0, c)

    return pl.pallas_call(
        functools.partial(_grad_kernel, v0, 1.0 / tokens),
        grid_spec=pltpu.PrefetchScalarGridSpec(
            num_scalar_prefetch=1,
            grid=(n_blocks // nb,),
            in_specs=[
                pl.BlockSpec((nb, sub, vp), at),
                pl.BlockSpec((hid, vp), lambda i, ids: (0, 0)),
                pl.BlockSpec((nb, STATS, sub), at_row),
                pl.BlockSpec((nb, 8, sub), at_row),
            ] + [pl.BlockSpec(memory_space=pl.ANY)] * len(extra),
            out_specs=[
                pl.BlockSpec((nb, sub, v0), at),
                pl.BlockSpec((nb, sub, vp - v0), at),
                pl.BlockSpec((1, nb, sub, hid), lambda i, ids: (lax.max(i - 2, 0), 0, 0, 0)),
                pl.BlockSpec((1, nb, sub, hid), lambda i, ids: (lax.min(i, 1), 0, 0, 0)),
            ],
        ),
        out_shape=[
            jax.ShapeDtypeStruct((n_blocks, rows, v0), jnp.bfloat16),
            jax.ShapeDtypeStruct((n_blocks, rows, vp - v0), jnp.bfloat16),
            jax.ShapeDtypeStruct((2, nb, sub, hid), jnp.float32),
            jax.ShapeDtypeStruct((2, nb, sub, hid), jnp.float32),
        ],
        input_output_aliases={5: 0, 6: 1} if extra else {},
        compiler_params=pltpu.CompilerParams(vmem_limit_bytes=VMEM_LIMIT),
        cost_estimate=pl.CostEstimate(flops=2 * n_blocks * sub * hid * vp, bytes_accessed=n_blocks * sub * vp * 6, transcendentals=n_blocks * sub * vp),
        name="grad_dx",
    )(ids, z, w, st, lab, *extra)


def _dw_call(xt, g):
    hid, tokens = xt.shape
    sub, width = g.shape[1:]
    kb = 1024
    steps = tokens // kb
    return pl.pallas_call(
        functools.partial(_dw_kernel, steps),
        grid=(steps,),
        in_specs=[
            pl.BlockSpec((hid, kb), lambda k: (0, k)),
            pl.BlockSpec((kb // sub, sub, width), lambda k: (k, 0, 0)),
        ],
        out_specs=pl.BlockSpec((hid, width), lambda k: (0, 0)),
        out_shape=jax.ShapeDtypeStruct((hid, width), jnp.bfloat16),
        scratch_shapes=[pltpu.VMEM((hid, width), jnp.float32)],
        compiler_params=pltpu.CompilerParams(vmem_limit_bytes=VMEM_LIMIT),
        cost_estimate=pl.CostEstimate(flops=2 * tokens * hid * width, bytes_accessed=tokens * (width + hid) * 2, transcendentals=0),
        name="dw",
    )(xt, g)


def _place_kernel(n_z, v0, zi_ref, *refs):
    o_ref = refs[-1]
    j = pl.program_id(0)
    dist = lax.rem(zi_ref[0] + n_z - j, n_z)
    for s in range(n_z):
        @pl.when(dist == s)
        def _():
            o_ref[:, :v0] = refs[2 * s][...]
            o_ref[:, v0:] = refs[2 * s + 1][...]


def _place_call(zi, pieces, vp, vocab_dev):
    n_z = len(pieces) // 2
    rows, v0 = pieces[0].shape
    return pl.pallas_call(
        functools.partial(_place_kernel, n_z, v0),
        grid=(n_z,),
        in_specs=[pl.BlockSpec(memory_space=pltpu.SMEM)]
        + [pl.BlockSpec(p.shape, lambda j: (0, 0)) for p in pieces],
        out_specs=pl.BlockSpec((rows, vp), lambda j: (0, j)),
        out_shape=jax.ShapeDtypeStruct((rows, vocab_dev), jnp.bfloat16),
        compiler_params=pltpu.CompilerParams(vmem_limit_bytes=VMEM_LIMIT),
        name="place",
    )(zi, *pieces)


def _after(value, *deps):
    return lax.optimization_barrier((value,) + deps)[0]


def solution(mesh):
    n_z = mesh.shape["fsdp"]
    n_tp = mesh.shape["tp"]
    n_blocks = n_z * n_tp
    token_spec = P(("dp", "fsdp", "tp"), None)
    label_spec = P(("dp", "fsdp", "tp"))

    def z_shift(a, s):
        return lax.ppermute(a, "fsdp", [(k, (k + s) % n_z) for k in range(n_z)])

    def swap(a, axis, bit):
        return lax.ppermute(a, axis, [(k, k ^ bit) for k in range(mesh.shape[axis])])

    def pick(a, i, axis=0):
        return lax.dynamic_index_in_dim(a, i, axis, keepdims=False)

    def step(hidden, w_head, labels):
        rows_dev, hid = hidden.shape
        w_rows, vocab_dev = w_head.shape
        tokens = rows_dev * n_blocks
        vp = _ceil_to(-(-vocab_dev // n_z), LANES)
        sub = rows_dev // CHUNKS
        zi = lax.axis_index("fsdp")
        tpi = lax.axis_index("tp")
        yi, ci = tpi // 2, tpi % 2

        w_pad = jnp.pad(w_head, ((0, 0), (0, n_z * vp - vocab_dev)))
        w_full, x_all, lab = _gather_call(w_pad, hidden, labels.reshape(1, rows_dev), vp, n_blocks)

        lab = lab - (tpi * vocab_dev + zi * vp)
        valid = jnp.minimum(vocab_dev - zi * vp, vp).astype(jnp.int32)
        lab = jnp.where((lab >= 0) & (lab < valid), lab, -1 - 2 * LANES).astype(jnp.float32)
        lab = jnp.broadcast_to(lab, (n_blocks, 8, rows_dev))

        z_all, local, xt = _logits_call(x_all, w_full, lab, valid.reshape(1))
        st = _stats_call(local)
        mean_loss = (jnp.sum(st[:, 2]) * (1.0 / tokens)).reshape(1)

        v0 = _tiles(vp)[2][0]
        ids = jnp.stack([ci, yi]).astype(jnp.int32)

        def grad(c, g_all, *deps):
            i = _after(ids, *deps) if deps else ids
            g0, g1, keep, send = _grad_call(c, i, z_all, w_full, st, lab, g_all, v0, sub)
            return (g0, g1), keep, swap(send, "tp", 1)

        def to_y(c, *deps):
            keep = _after(keeps[c], *deps)
            other = keep[1] + gots[c][1]
            mine = keep[0] + gots[c][0]
            ys[c] = (mine, swap(other, "tp", 2))
            return mine, other

        def to_near(c, *deps):
            both = (_after(ys[c][0], *deps) + ys[c][1]).reshape(2, 2, sub, hid)
            odd = zi % 2
            mine, other = pick(both, odd, 1), pick(both, 1 - odd, 1)
            nears[c] = (mine, swap(other, "fsdp", 1))
            return mine, other

        def to_far(c, *deps):
            both = _after(nears[c][0], *deps) + nears[c][1]
            high = zi // 2
            mine, other = pick(both, high), pick(both, 1 - high)
            fars[c] = (mine, swap(other, "fsdp", 2))
            return mine, other

        def last(c, *deps):
            return (_after(fars[c][0], *deps) + fars[c][1]).astype(jnp.bfloat16)

        def send_dw(dw):
            parts = [pick(dw, (zi + s) % n_z) for s in range(n_z)]
            sent = [parts[0]]
            for s in range(1, n_z):
                sent.append(z_shift(parts[s], s))
            return parts, sent

        keeps, gots, ys, nears, fars = ([None] * CHUNKS for _ in range(5))
        g, keeps[0], gots[0] = grad(0, None)
        g, keeps[1], gots[1] = grad(1, g, keeps[0])
        t = to_y(0, keeps[1])
        g, keeps[2], gots[2] = grad(2, g, *t)
        t = to_y(1, keeps[2])
        g, keeps[3], gots[3] = grad(3, g, *t)
        t = to_y(2, keeps[3]) + to_near(0, keeps[3])
        dw0 = _dw_call(_after(xt, *t), g[0]).reshape(n_z, w_rows, v0)
        parts0, pieces0 = send_dw(dw0)
        t = to_y(3, dw0) + to_near(1, dw0) + to_far(0, dw0) + tuple(parts0)
        dw1 = _dw_call(_after(xt, *t), g[1]).reshape(n_z, w_rows, vp - v0)
        parts1, pieces1 = send_dw(dw1)
        t = to_near(2, *parts1)
        t = to_far(1, *t)
        t = to_near(3, *t)
        t = to_far(2, *t)
        t = to_far(3, *t)
        out = [last(c, *t) for c in range(CHUNKS)]
        pieces = [p for pair in zip(pieces0, pieces1) for p in pair]
        zv = _after(zi.reshape(1).astype(jnp.int32), *out)
        d_w = _place_call(zv, pieces, vp, vocab_dev)
        return mean_loss, jnp.concatenate(out, axis=0), d_w

    return jax.shard_map(
        step,
        mesh=mesh,
        in_specs=(token_spec, P("fsdp", "tp"), label_spec),
        out_specs=(P("dp"), token_spec, P(("dp", "fsdp"), "tp")),
        check_vma=False,
    )
```

time: 1330 us -> 605 us (0.45)
  waiting for transfers between devices: 983 us -> 144 us
  Pallas kernels: 0 us -> 350 us
  matrix products: 151 us -> 0 us
  other arithmetic: 85.4 us -> 31 us
  starting transfers between devices: 0.38 us -> 47.1 us
  local copies, waits for them, and re-layouts: 56.9 us -> 19.4 us
  blocking collectives: 33.7 us -> 0 us
    unnamed x5 -> x0, waiting for transfers between devices: 623 us -> none
    all_gather x2 -> x0, waiting for transfers between devices: 360 us -> none  [the longest x1 335 us: local_step(): w_full = lax.all_gather(w_head, 'fsdp', axis=0, tiled=True)]
    pallas_call x0 -> x10, Pallas kernels: none -> 350 us  [the longest x1 125 us: _gather_call(): pl.pallas_call(_gather_kernel, in_specs=[pl.BlockSpec(memory_space=pl.ANY...]
    dot_general x3 -> x0, matrix products: 151 us -> none  [the longest x1 51.5 us: local_step(): jnp.einsum('tv,hv->th', grad_logits, w_full, preferred_element_type=jnp.f...]
    ppermute x0 -> x22, waiting for transfers between devices: none -> 144 us  [the longest x16 121 us: swap(): lax.ppermute(a, axis, [(k, k ^ bit) for k in range(mesh.shape[axis])])]
    unnamed x15 -> x27, local copies, waits for them, and re-layouts: 56.3 us -> 2.92 us
    convert_element_type x2 -> x5, other arithmetic: 52.6 us -> 1.98 us  [the longest x4 1.17 us: last(): return (_after(fars[c][0], *deps) + fars[c][1]).astype(jnp.bfloat16)]
    ppermute x0 -> x22, starting transfers between devices: none -> 47.1 us  [the longest x6 32 us: z_shift(): return lax.ppermute(a, 'fsdp', [(k, (k + s) % n_z) for k in range(n_z)])]
  transfers between devices with their start and end apart: 4 -> 22, of which waited for: 3 -> 6; matrix products, arithmetic and copies ran while one was open for 7% -> 7% of each run, Pallas kernels for 0% -> 21%
where the time goes in v1:
time: 605 us; the launch traced here: 594 us
  Pallas kernels  350 us (58%)
  waiting for transfers between devices  144 us (24%)
  starting transfers between devices  47.1 us (8%)
  other arithmetic  31 us (5%)
  local copies, waits for them, and re-layouts  19.4 us (3%)
    pallas_call x1, Pallas kernels, _gather_call(): pl.pallas_call(_gather_kernel, in_specs=[pl.BlockSpec(memory_space=pl.ANY...  125 us
    ppermute x16, waiting for transfers between devices, swap(): lax.ppermute(a, axis, [(k, k ^ bit) for k in range(mesh.shape[axis])])  121 us
    pallas_call x4, Pallas kernels, _grad_call(): pl.pallas_call(functools.partial(_grad_kernel, v0, 1.0 / tokens), grid_sp...  92.2 us
    pallas_call x1, Pallas kernels, _logits_call(): pl.pallas_call(functools.partial(_logits_kernel, vp), grid=(n_blocks,), i...  59.6 us
    pallas_call x2, Pallas kernels, _dw_call(): pl.pallas_call(functools.partial(_dw_kernel, steps), grid=(steps,), in_sp...  53.9 us
    ppermute x6, starting transfers between devices, z_shift(): return lax.ppermute(a, 'fsdp', [(k, (k + s) % n_z) for k in range(n_z)])  32 us
    ppermute x6, waiting for transfers between devices, z_shift(): return lax.ppermute(a, 'fsdp', [(k, (k + s) % n_z) for k in range(n_z)])  23.4 us
    add x4, other arithmetic, to_y(): other = keep[1] + gots[c][1]  15.8 us
  transfers between devices with their start and end apart: 22, of which 6 were waited for; matrix products, arithmetic and copies ran while one was open for 7% of the time, Pallas kernels for 21%

profile of v1, /device:TPU:0, one launch (start us, length us, event | category | flops | bytes accessed | tf_op | source)
XLA Modules:
  0.0 594.1 jit_solution(2934372472019973318)
XLA Ops:
  0.7 4.9 pad.4.w_ref
  5.5 124.9 %gather.1 = (bf16[768,3200]{1,0:T(8,128)(2,1)}, bf16[16,512,768]{2,1,0:T(8,128)(2,1)}, s32[16,1,512]{2,1,0:T(1,128)}) custom-call(bf16[192,12800]{1,0:T(8,128)(2,1)} %pad.4.w_ref, bf16[512,768]{1,0:T(8,128)(2,1)} %x_ref.1, s32[1,512]{1,0:T(1,128)} %bitcast.86), custom_call_target="tpu_custom_call" | custom-call | tf_op jit(solution)/shard_map/gather/pallas_call | solution.py:231
  132.0 59.6 %logits_stats.1 = (f32[16,512,3200]{2,1,0:T(8,128)}, f32[16,4,512]{2,1,0:T(4,128)}, bf16[768,8192]{1,0:T(8,128)(2,1)}) custom-call(s32[1]{0:T(128)} %bitcast.valid_ref, bf16[16,512,768]{2,1,0:T(8,128)(2,1)} %get-tuple-element.47.x_ref, bf16[768,3200]{1,0:T(8,128)(2,1)} %get-tuple-element.48.w_ref, f32[16,8,512]{2,1,0:T(8,128)} %broadcast_in_dim.13.lab_ref), custom_call_target="tpu_custom_call" | custom-call | flops 40265318400 | bytes 104857600 | tf_op jit(solution)/shard_map/logits_stats/pallas_call | solution.py:314
  191.6 14.0 %stats.1.st_ref = f32[16,4,512]{2,1,0:T(4,128)} custom-call(f32[16,4,512]{2,1,0:T(4,128)} %get-tuple-element.50.st_ref), custom_call_target="tpu_custom_call" | custom-call | tf_op jit(solution)/shard_map/stats/pallas_call | solution.py:299
  206.3 23.0 %grad_dx.4 = (bf16[16,512,1536]{2,1,0:T(8,128)(2,1)}, bf16[16,512,1664]{2,1,0:T(8,128)(2,1)}, f32[2,4,128,768]{3,2,1,0:T(8,128)}, f32[2,4,128,768]{3,2,1,0:T(8,128)}) custom-call(s32[2]{0:T(128)} %pad_add_fusion.ids_ref, f32[16,512,3200]{2,1,0:T(8,128)} %get-tuple-element.51.z_ref, bf16[768,3200]{1,0:T(8,128)(2,1)} %get-tuple-element.48.w_ref, ...), custom_call_target="tpu_custom_call" | custom-call | flops 10066329600 | bytes 39321600 | tf_op jit(solution)/shard_map/grad_dx/pallas_call | solution.py:358
  229.3 23.0 %grad_dx.5 = (bf16[16,512,1536]{2,1,0:T(8,128)(2,1)}, bf16[16,512,1664]{2,1,0:T(8,128)(2,1)}, f32[2,4,128,768]{3,2,1,0:T(8,128)}, f32[2,4,128,768]{3,2,1,0:T(8,128)}) custom-call(s32[2]{0:T(128)} %pad_add_fusion.ids_ref, f32[16,512,3200]{2,1,0:T(8,128)} %get-tuple-element.51.z_ref, ...), custom_call_target="tpu_custom_call", output_to_operand_aliasing={{0}: (5, {}), {1}: (6, {})} | custom-call | flops 10066329600 | bytes 39321600 | tf_op jit(solution)/shard_map/grad_dx/pallas_call | solution.py:358
  252.7 4.4 fusion.6
  257.2 23.2 %grad_dx.6 = (bf16[16,512,1536]{2,1,0:T(8,128)(2,1)}, bf16[16,512,1664]{2,1,0:T(8,128)(2,1)}, f32[2,4,128,768]{3,2,1,0:T(8,128)}, f32[2,4,128,768]{3,2,1,0:T(8,128)}) custom-call(s32[2]{0:T(128)} %pad_add_fusion.ids_ref, f32[16,512,3200]{2,1,0:T(8,128)} %get-tuple-element.51.z_ref, ...), custom_call_target="tpu_custom_call", output_to_operand_aliasing={{0}: (5, {}), {1}: (6, {})} | custom-call | flops 10066329600 | bytes 39321600 | tf_op jit(solution)/shard_map/grad_dx/pallas_call | solution.py:358
  281.4 4.4 fusion.4
  285.9 23.0 %grad_dx.7 = (bf16[16,512,1536]{2,1,0:T(8,128)(2,1)}, bf16[16,512,1664]{2,1,0:T(8,128)(2,1)}, f32[2,4,128,768]{3,2,1,0:T(8,128)}, f32[2,4,128,768]{3,2,1,0:T(8,128)}) custom-call(s32[2]{0:T(128)} %pad_add_fusion.ids_ref, f32[16,512,3200]{2,1,0:T(8,128)} %get-tuple-element.51.z_ref, ...), custom_call_target="tpu_custom_call", output_to_operand_aliasing={{0}: (5, {}), {1}: (6, {})} | custom-call | flops 10066329600 | bytes 39321600 | tf_op jit(solution)/shard_map/grad_dx/pallas_call | solution.py:358
  310.1 8.0 %collective-permute-done.2 = f32[4,128,768]{2,1,0:T(8,128)} collective-permute-done((f32[4,128,768]{2,1,0:T(8,128)}, f32[4,128,768]{2,1,0:T(8,128)}, u32[]{:S(2)}, u32[]{:S(2)}) %collective-permute-start.2) | collective-permute-done | bytes 1572896 | tf_op jit(solution)/shard_map/ppermute | solution.py:451
  322.1 3.5 fusion.2
  325.6 25.2 %dw.2 = bf16[768,1536]{1,0:T(8,128)(2,1)} custom-call(bf16[768,8192]{1,0:T(8,128)(2,1)} %get-tuple-element.79.xt_ref, bf16[16,512,1536]{2,1,0:T(8,128)(2,1)} %get-tuple-element.74.g_ref), custom_call_target="tpu_custom_call" | custom-call | flops 19327352832 | bytes 37748736 | tf_op jit(solution)/shard_map/dw/pallas_call | solution.py:394
  355.8 3.4 fusion
  363.8 28.7 %dw.3 = bf16[768,1664]{1,0:T(8,128)(2,1)} custom-call(bf16[768,8192]{1,0:T(8,128)(2,1)} %get-tuple-element.79.xt_ref, bf16[16,512,1664]{2,1,0:T(8,128)(2,1)} %get-tuple-element.80.g_ref), custom_call_target="tpu_custom_call" | custom-call | flops 20937965568 | bytes 39845888 | tf_op jit(solution)/shard_map/dw/pallas_call | solution.py:394
  392.5 3.2 dynamic-slice_bitcast_fusion.8
  401.2 19.0 %collective-permute-done.9 = f32[4,128,768]{2,1,0:T(8,128)} collective-permute-done((f32[4,128,768]{2,1,0:T(8,128)}, f32[4,128,768]{2,1,0:T(8,128)}, u32[]{:S(2)}, u32[]{:S(2)}) %collective-permute-start.9) | collective-permute-done | bytes 1572896 | tf_op jit(solution)/shard_map/ppermute | solution.py:451
  432.1 50.8 %collective-permute-done.11 = f32[2,128,768]{2,1,0:T(8,128)} collective-permute-done((f32[2,128,768]{2,1,0:T(8,128)}, f32[2,128,768]{2,1,0:T(8,128)}, u32[]{:S(2)}, u32[]{:S(2)}) %collective-permute-start.11) | collective-permute-done | bytes 786464 | tf_op jit(solution)/shard_map/ppermute | solution.py:451
  484.3 2.9 collective-permute-start.15
  490.3 34.5 %collective-permute-done.14 = f32[128,768]{1,0:T(8,128)S(1)} collective-permute-done((f32[128,768]{1,0:T(8,128)S(1)}, f32[128,768]{1,0:T(8,128)S(1)}, u32[]{:S(2)}, u32[]{:S(2)}) %collective-permute-start.14) | collective-permute-done | bytes 393248 | tf_op jit(solution)/shard_map/ppermute | solution.py:451
  524.8 8.4 %collective-permute-done.15 = f32[128,768]{1,0:T(8,128)S(1)} collective-permute-done((f32[128,768]{1,0:T(8,128)S(1)}, f32[128,768]{1,0:T(8,128)S(1)}, u32[]{:S(2)}, u32[]{:S(2)}) %collective-permute-start.15) | collective-permute-done | bytes 393248 | tf_op jit(solution)/shard_map/ppermute | solution.py:451
  533.2 28.3 %collective-permute-start.20 = (bf16[192,1536]{1,0:T(8,128)(2,1)S(1)}, bf16[192,1536]{1,0:T(8,128)(2,1)S(1)}, u32[]{:S(2)}, u32[]{:S(2)}) collective-permute-start(bf16[192,1536]{1,0:T(8,128)(2,1)S(1)} %copy-done.11), channel_id=1, source_target_pairs={{0,12},{4,0},{8,4},{12,8},{1,13},{5,1},{9,5},{13,9},{2,14},{6,2},{... | collective-permute-start | bytes 1769480 | tf_op jit(solution)/shard_map/ppermute | solution.py:448
  562.5 23.4 %collective-permute-done.18.refs_4_ = bf16[192,1536]{1,0:T(8,128)(2,1)S(1)} collective-permute-done((bf16[192,1536]{1,0:T(8,128)(2,1)S(1)}, bf16[192,1536]{1,0:T(8,128)(2,1)S(1)}, u32[]{:S(2)}, u32[]{:S(2)}) %collective-permute-start.18) | collective-permute-done | bytes 589856 | tf_op jit(solution)/shard_map/ppermute | solution.py:448
  587.9 5.0 place.1
  (89 shorter events, 42.7 us)
Async XLA Ops:
  229.3 23.4 %collective-permute-start = (f32[2,4,128,768]{3,2,1,0:T(8,128)}, f32[2,4,128,768]{3,2,1,0:T(8,128)}, u32[]{:S(2)}, u32[]{:S(2)}) collective-permute-start(f32[2,4,128,768]{3,2,1,0:T(8,128)} %get-tuple-element.58), channel_id=1, source_target_pairs={{0,1},{1,0},{2,3},{3,2},{4,5},{5,4},{6,7},{7,6},{8,9},{9,8},{10,11... | collective-permute-start | bytes 9437192 | tf_op jit(solution)/shard_map/ppermute | solution.py:451
  252.3 29.1 %collective-permute-start.1 = (f32[2,4,128,768]{3,2,1,0:T(8,128)}, f32[2,4,128,768]{3,2,1,0:T(8,128)}, u32[]{:S(2)}, u32[]{:S(2)}) collective-permute-start(f32[2,4,128,768]{3,2,1,0:T(8,128)} %get-tuple-element.64), channel_id=1, source_target_pairs={{0,1},{1,0},{2,3},{3,2},{4,5},{5,4},{6,7},{7,6},{8,9},{9,8},{10,11... | collective-permute-start | bytes 9437192 | tf_op jit(solution)/shard_map/ppermute | solution.py:451
  280.4 41.2 %collective-permute-start.3 = (f32[2,4,128,768]{3,2,1,0:T(8,128)}, f32[2,4,128,768]{3,2,1,0:T(8,128)}, u32[]{:S(2)}, u32[]{:S(2)}) collective-permute-start(f32[2,4,128,768]{3,2,1,0:T(8,128)} %get-tuple-element.72), channel_id=1, source_target_pairs={{0,1},{1,0},{2,3},{3,2},{4,5},{5,4},{6,7},{7,6},{8,9},{9,8},{10,11... | collective-permute-start | bytes 9437192 | tf_op jit(solution)/shard_map/ppermute | solution.py:451
  280.5 37.6 %collective-permute-start.2 = (f32[4,128,768]{2,1,0:T(8,128)}, f32[4,128,768]{2,1,0:T(8,128)}, u32[]{:S(2)}, u32[]{:S(2)}) collective-permute-start(f32[4,128,768]{2,1,0:T(8,128)} %get-tuple-element.97), channel_id=1, source_target_pairs={{0,2},{1,3},{2,0},{3,1},{4,6},{5,7},{6,4},{7,5},{8,10},{9,11},{10,... | collective-permute-start | bytes 4718600 | tf_op jit(solution)/shard_map/ppermute | solution.py:451
  308.9 46.7 %collective-permute-start.5 = (f32[2,4,128,768]{3,2,1,0:T(8,128)}, f32[2,4,128,768]{3,2,1,0:T(8,128)}, u32[]{:S(2)}, u32[]{:S(2)}) collective-permute-start(f32[2,4,128,768]{3,2,1,0:T(8,128)} %get-tuple-element.77), channel_id=1, source_target_pairs={{0,1},{1,0},{2,3},{3,2},{4,5},{5,4},{6,7},{7,6},{8,9},{9,8},{10,11... | collective-permute-start | bytes 9437192 | tf_op jit(solution)/shard_map/ppermute | solution.py:451
  308.9 42.8 %collective-permute-start.6 = (f32[4,128,768]{2,1,0:T(8,128)}, f32[4,128,768]{2,1,0:T(8,128)}, u32[]{:S(2)}, u32[]{:S(2)}) collective-permute-start(f32[4,128,768]{2,1,0:T(8,128)} %get-tuple-element.95), channel_id=1, source_target_pairs={{0,2},{1,3},{2,0},{3,1},{4,6},{5,7},{6,4},{7,5},{8,10},{9,11},{10,... | collective-permute-start | bytes 4718600 | tf_op jit(solution)/shard_map/ppermute | solution.py:451
  320.9 39.4 %collective-permute-start.4 = (f32[2,128,768]{2,1,0:T(8,128)}, f32[2,128,768]{2,1,0:T(8,128)}, u32[]{:S(2)}, u32[]{:S(2)}) collective-permute-start(f32[2,128,768]{2,1,0:T(8,128)} %get-tuple-element.113), channel_id=1, source_target_pairs={{0,4},{4,0},{8,12},{12,8},{1,5},{5,1},{9,13},{13,9},{2,6},{6,2},{1... | collective-permute-start | bytes 2359304 | tf_op jit(solution)/shard_map/ppermute | solution.py:451
  350.8 44.9 %collective-permute-start.7 = (f32[4,128,768]{2,1,0:T(8,128)}, f32[4,128,768]{2,1,0:T(8,128)}, u32[]{:S(2)}, u32[]{:S(2)}) collective-permute-start(f32[4,128,768]{2,1,0:T(8,128)} %get-tuple-element.93), channel_id=1, source_target_pairs={{0,2},{1,3},{2,0},{3,1},{4,6},{5,7},{6,4},{7,5},{8,10},{9,11},{10,... | collective-permute-start | bytes 4718600 | tf_op jit(solution)/shard_map/ppermute | solution.py:451
  354.7 44.5 %collective-permute-start.8 = (f32[2,128,768]{2,1,0:T(8,128)}, f32[2,128,768]{2,1,0:T(8,128)}, u32[]{:S(2)}, u32[]{:S(2)}) collective-permute-start(f32[2,128,768]{2,1,0:T(8,128)} %get-tuple-element.111), channel_id=1, source_target_pairs={{0,4},{4,0},{8,12},{12,8},{1,5},{5,1},{9,13},{13,9},{2,6},{6,2},{1... | collective-permute-start | bytes 2359304 | tf_op jit(solution)/shard_map/ppermute | solution.py:451
  359.3 60.9 %collective-permute-start.9 = (f32[4,128,768]{2,1,0:T(8,128)}, f32[4,128,768]{2,1,0:T(8,128)}, u32[]{:S(2)}, u32[]{:S(2)}) collective-permute-start(f32[4,128,768]{2,1,0:T(8,128)} %get-tuple-element.91), channel_id=1, source_target_pairs={{0,2},{1,3},{2,0},{3,1},{4,6},{5,7},{6,4},{7,5},{8,10},{9,11},{10,... | collective-permute-start | bytes 4718600 | tf_op jit(solution)/shard_map/ppermute | solution.py:451
  398.3 30.9 %collective-permute-start.10 = (f32[2,128,768]{2,1,0:T(8,128)}, f32[2,128,768]{2,1,0:T(8,128)S(1)}, u32[]{:S(2)}, u32[]{:S(2)}) collective-permute-start(f32[2,128,768]{2,1,0:T(8,128)} %get-tuple-element.109), channel_id=1, source_target_pairs={{0,4},{4,0},{8,12},{12,8},{1,5},{5,1},{9,13},{13,9},{2,6},{6,2},{1... | collective-permute-start | bytes 2359304 | tf_op jit(solution)/shard_map/ppermute | solution.py:451
  422.8 60.1 %collective-permute-start.11 = (f32[2,128,768]{2,1,0:T(8,128)}, f32[2,128,768]{2,1,0:T(8,128)}, u32[]{:S(2)}, u32[]{:S(2)}) collective-permute-start(f32[2,128,768]{2,1,0:T(8,128)} %get-tuple-element.107), channel_id=1, source_target_pairs={{0,4},{4,0},{8,12},{12,8},{1,5},{5,1},{9,13},{13,9},{2,6},{6,2},{1... | collective-permute-start | bytes 2359304 | tf_op jit(solution)/shard_map/ppermute | solution.py:451
  423.5 60.8 %collective-permute-start.12 = (f32[128,768]{1,0:T(8,128)}, f32[128,768]{1,0:T(8,128)}, u32[]{:S(2)}, u32[]{:S(2)}) collective-permute-start(f32[128,768]{1,0:T(8,128)} %get-tuple-element.121), channel_id=1, source_target_pairs={{0,8},{4,12},{8,0},{12,4},{1,9},{5,13},{9,1},{13,5},{2,10},{6,14},... | collective-permute-start | bytes 1179656 | tf_op jit(solution)/shard_map/ppermute | solution.py:451
  425.2 63.0 %collective-permute-start.16 = (bf16[192,1536]{1,0:T(8,128)(2,1)}, bf16[192,1536]{1,0:T(8,128)(2,1)}, u32[]{:S(2)}, u32[]{:S(2)}) collective-permute-start(bf16[192,1536]{1,0:T(8,128)(2,1)} %get-tuple-element.105), channel_id=1, source_target_pairs={{0,4},{4,8},{8,12},{12,0},{1,5},{5,9},{9,13},{13,1},{2,6},{6,10},{... | collective-permute-start | bytes 1769480 | tf_op jit(solution)/shard_map/ppermute | solution.py:448
  428.0 157.8 %collective-permute-start.17 = (bf16[192,1664]{1,0:T(8,128)(2,1)}, bf16[192,1664]{1,0:T(8,128)(2,1)}, u32[]{:S(2)}, u32[]{:S(2)}) collective-permute-start(bf16[192,1664]{1,0:T(8,128)(2,1)} %get-tuple-element.101), channel_id=1, source_target_pairs={{0,4},{4,8},{8,12},{12,0},{1,5},{5,9},{9,13},{13,1},{2,6},{6,10},{... | collective-permute-start | bytes 1916936 | tf_op jit(solution)/shard_map/ppermute | solution.py:448
  429.2 59.2 %collective-permute-start.13 = (f32[128,768]{1,0:T(8,128)}, f32[128,768]{1,0:T(8,128)S(1)}, u32[]{:S(2)}, u32[]{:S(2)}) collective-permute-start(f32[128,768]{1,0:T(8,128)} %get-tuple-element.119), channel_id=1, source_target_pairs={{0,8},{4,12},{8,0},{12,4},{1,9},{5,13},{9,1},{13,5},{2,10},{6,14},... | collective-permute-start | bytes 1179656 | tf_op jit(solution)/shard_map/ppermute | solution.py:451
  484.1 40.7 %copy-start.12 = (bf16[192,1536]{1,0:T(8,128)(2,1)S(1)}, bf16[192,1536]{1,0:T(8,128)(2,1)}, u32[]{:S(2)}) copy-start(bf16[192,1536]{1,0:T(8,128)(2,1)} %get-tuple-element.104) | copy-start | bytes 1769476
  484.1 49.1 %copy-start.11 = (bf16[192,1536]{1,0:T(8,128)(2,1)S(1)}, bf16[192,1536]{1,0:T(8,128)(2,1)}, u32[]{:S(2)}) copy-start(bf16[192,1536]{1,0:T(8,128)(2,1)} %get-tuple-element.103) | copy-start | bytes 1769476
  484.2 40.6 %collective-permute-start.14 = (f32[128,768]{1,0:T(8,128)S(1)}, f32[128,768]{1,0:T(8,128)S(1)}, u32[]{:S(2)}, u32[]{:S(2)}) collective-permute-start(f32[128,768]{1,0:T(8,128)S(1)} %get-tuple-element.117), channel_id=1, source_target_pairs={{0,8},{4,12},{8,0},{12,4},{1,9},{5,13},{9,1},{13,5},{2,10},{6,14},... | collective-permute-start | bytes 1179656 | tf_op jit(solution)/shard_map/ppermute | solution.py:451
  484.3 48.9 %collective-permute-start.15 = (f32[128,768]{1,0:T(8,128)S(1)}, f32[128,768]{1,0:T(8,128)S(1)}, u32[]{:S(2)}, u32[]{:S(2)}) collective-permute-start(f32[128,768]{1,0:T(8,128)S(1)} %get-tuple-element.115), channel_id=1, source_target_pairs={{0,8},{4,12},{8,0},{12,4},{1,9},{5,13},{9,1},{13,5},{2,10},{6,14},... | collective-permute-start | bytes 1179656 | tf_op jit(solution)/shard_map/ppermute | solution.py:451
  488.3 97.6 %collective-permute-start.19 = (bf16[192,1664]{1,0:T(8,128)(2,1)S(1)}, bf16[192,1664]{1,0:T(8,128)(2,1)S(1)}, u32[]{:S(2)}, u32[]{:S(2)}) collective-permute-start(bf16[192,1664]{1,0:T(8,128)(2,1)S(1)} %copy-done.8), channel_id=1, source_target_pairs={{0,8},{4,12},{8,0},{12,4},{1,9},{5,13},{9,1},{13,5},{2,10},{6,14},... | collective-permute-start | bytes 1916936 | tf_op jit(solution)/shard_map/ppermute | solution.py:448
  488.4 97.5 %collective-permute-start.21 = (bf16[192,1664]{1,0:T(8,128)(2,1)S(1)}, bf16[192,1664]{1,0:T(8,128)(2,1)S(1)}, u32[]{:S(2)}, u32[]{:S(2)}) collective-permute-start(bf16[192,1664]{1,0:T(8,128)(2,1)S(1)} %copy-done.7), channel_id=1, source_target_pairs={{0,12},{4,0},{8,4},{12,8},{1,13},{5,1},{9,5},{13,9},{2,14},{6,2},{... | collective-permute-start | bytes 1916936 | tf_op jit(solution)/shard_map/ppermute | solution.py:448
  524.8 61.1 %collective-permute-start.18 = (bf16[192,1536]{1,0:T(8,128)(2,1)S(1)}, bf16[192,1536]{1,0:T(8,128)(2,1)S(1)}, u32[]{:S(2)}, u32[]{:S(2)}) collective-permute-start(bf16[192,1536]{1,0:T(8,128)(2,1)S(1)} %copy-done.12), channel_id=1, source_target_pairs={{0,8},{4,12},{8,0},{12,4},{1,9},{5,13},{9,1},{13,5},{2,10},{6,14},... | collective-permute-start | bytes 1769480 | tf_op jit(solution)/shard_map/ppermute | solution.py:448
  533.2 52.7 %collective-permute-start.20 = (bf16[192,1536]{1,0:T(8,128)(2,1)S(1)}, bf16[192,1536]{1,0:T(8,128)(2,1)S(1)}, u32[]{:S(2)}, u32[]{:S(2)}) collective-permute-start(bf16[192,1536]{1,0:T(8,128)(2,1)S(1)} %copy-done.11), channel_id=1, source_target_pairs={{0,12},{4,0},{8,4},{12,8},{1,13},{5,1},{9,5},{13,9},{2,14},{6,2},{... | collective-permute-start | bytes 1769480 | tf_op jit(solution)/shard_map/ppermute | solution.py:448
  (11 other events, 27.9 us)

commit v2 on v1

--- a/solution.py
+++ b/solution.py
@@ -31,12 +31,12 @@
     return list(zip(edges[:-1], edges[1:]))
 
 
-def _logits_kernel(vp, valid_ref, x_ref, w_ref, lab_ref, z_ref, st_ref, xt_ref, m_ref, s_ref, t_ref, l_ref):
-    rows, _ = x_ref.shape[1:]
-    valid = valid_ref[0]
-    x = x_ref[0]
+def _logits_block(x, w_ref, lab_row, valid, z_ref, xt_ref, m_ref, s_ref, t_ref, l_ref):
+    rows = x.shape[0]
+    vp = w_ref.shape[1]
     lane = lax.broadcasted_iota(jnp.int32, (rows, LANES), 1)
-    l_ref[...] = _rows_to_cols(lab_ref)[:, 0:1].astype(jnp.int32) - lane
+    lab = jnp.broadcast_to(lab_row.astype(jnp.float32), (LANES, rows)).T
+    l_ref[...] = lab.astype(jnp.int32) - lane
     m_ref[...] = jnp.full((rows, LANES), NEG, jnp.float32)
     s_ref[...] = jnp.zeros((rows, LANES), jnp.float32)
     t_ref[...] = jnp.zeros((rows, LANES), jnp.float32)
@@ -45,7 +45,7 @@
     def stats(c0, c1):
         for r in range(0, rows, step):
             sl = slice(r, r + step)
-            zs = [z_ref[0, sl, k:k + LANES] for k in range(c0, c1, LANES)]
+            zs = [z_ref[sl, k:k + LANES] for k in range(c0, c1, LANES)]
             off = l_ref[sl, :]
             t = t_ref[sl, :]
             m_old = m_ref[sl, :]
@@ -65,11 +65,11 @@
         z = jnp.dot(x, w_ref[:, c0:c1], preferred_element_type=jnp.float32)
         if c1 == vp:
             edge = (vp - 2 * LANES - c0) // LANES * LANES
-            z_ref[0, :, c0:c0 + edge] = z[:, :edge]
+            z_ref[:, c0:c0 + edge] = z[:, :edge]
             for k in range(edge, c1 - c0, LANES):
-                z_ref[0, :, c0 + k:c0 + k + LANES] = jnp.where(lane < valid - (c0 + k), z[:, k:k + LANES], NEG)
+                z_ref[:, c0 + k:c0 + k + LANES] = jnp.where(lane < valid - (c0 + k), z[:, k:k + LANES], NEG)
         else:
-            z_ref[0, :, c0:c1] = z
+            z_ref[:, c0:c1] = z
         if before is not None:
             stats(*before)
         before = (c0, c1)
@@ -80,7 +80,7 @@
     s_row = jnp.sum(s_ref[...] * jnp.exp(m - m_row), axis=1, keepdims=True)
     t_row = jnp.sum(t_ref[...], axis=1, keepdims=True)
     packed = jnp.where(lane == 0, m_row, jnp.where(lane == 1, s_row, t_row))
-    st_ref[0] = packed.T[0:STATS, :]
+    return packed.T[0:STATS, :]
 
 
 def _grad_kernel(v0, inv_tokens, ids_ref, z_ref, w_ref, st_ref, lab_ref, *rest):
@@ -129,25 +129,31 @@
         o_ref[...] = acc_ref[...].astype(o_ref.dtype)
 
 
-def _gather_kernel(w_ref, x_ref, l_ref, wf_ref, xf_ref, lf_ref, w_buf, x_buf, l_buf, loc,
-                   w_s, w_r, wx_s, wx_r, x_s, x_r, y_s, y_r, c_s, c_r, l_s, l_r):
+def _front_kernel(vocab_dev, w_ref, x_ref, l_ref, wo_ref, lo_ref, zo_ref, xto_ref, st_ref,
+                  wv, xv, lv, zb, xtb, ms, ss, ts, ls, loc, z_sem, xt_sem,
+                  w_s, w_r, wx_s, wx_r, x_s, x_r, y_s, y_r, c_s, c_r, l_s, l_r):
     n_z, n_tp = 4, 4
     n = n_z * n_tp
     dp, zi, tp = lax.axis_index("dp"), lax.axis_index("fsdp"), lax.axis_index("tp")
     w_rows = w_ref.shape[0]
     half = w_rows // 2
-    vp = wf_ref.shape[1]
+    vp = wv.shape[1]
+    rows = x_ref.shape[0]
     mine = tp * n_z + zi
 
     def dev(p):
         return (dp, lax.rem(p, n_z), lax.div(p, n_z))
 
+    def flip(v, j):
+        high = lax.rem(lax.div(v, 2) + j // 2, 2)
+        low = lax.rem(lax.rem(v, 2) + lax.rem(j, 2), 2)
+        return high * 2 + low
+
     peers = [dev(lax.rem(mine + o, n)) for o in range(n)]
-    y_tp, c_tp = lax.rem(tp + 2, n_tp), tp + 1 - 2 * lax.rem(tp, 2)
+    y_tp, c_tp = flip(tp, 2), flip(tp, 1)
     y_dev, c_dev, x_dev = (dp, zi, y_tp), (dp, zi, c_tp), (1 - dp, zi, tp)
-    near, far, third = zi + 1 - 2 * lax.rem(zi, 2), lax.rem(zi + 2, n_z), n_z - 1 - zi
-    z_owner = [zi, near, far, third]
-    near_dev, far_dev = (dp, near, tp), (dp, far, tp)
+    z_owner = [flip(zi, j) for j in range(n_z)]
+    near_dev, far_dev = (dp, z_owner[1], tp), (dp, z_owner[2], tp)
 
     barrier = pltpu.get_barrier_semaphore()
     for d in peers[1:] + [x_dev]:
@@ -158,93 +164,149 @@
         return pltpu.make_async_remote_copy(src, dst, s_sem, r_sem, device_id=d, device_id_type=MESH)
 
     def w_half(owner, part):
-        return wf_ref.at[pl.ds(pl.multiple_of(owner * w_rows + part * half, 8), half), :]
+        return wv.at[pl.ds(pl.multiple_of(owner * w_rows + part * half, 8), half), :]
 
     def w_cols(z):
         return pl.ds(pl.multiple_of(z * vp, LANES), vp)
 
-    sends = []
-
-    def go(copy):
-        copy.start()
-        sends.append(copy)
-        return copy
-
-    load_x = pltpu.make_async_copy(x_ref, x_buf, loc.at[0])
-    load_w = pltpu.make_async_copy(w_ref.at[:, w_cols(zi)], w_buf, loc.at[1])
-    load_l = pltpu.make_async_copy(l_ref, l_buf, loc.at[2])
+    load_x = pltpu.make_async_copy(x_ref, xv.at[mine], loc.at[0])
+    load_w = pltpu.make_async_copy(w_ref.at[:, w_cols(zi)], wv.at[pl.ds(pl.multiple_of(zi * w_rows, 8), w_rows), :], loc.at[1])
+    load_l = pltpu.make_async_copy(l_ref, lv.at[mine], loc.at[2])
     load_x.start()
     load_w.start()
     load_l.start()
-    x_in = [None] * n_z
-    x_in[2] = go(remote(x_ref, xf_ref.at[mine], x_s.at[2], x_r.at[2], far_dev))
-    x_in[1] = go(remote(x_ref, xf_ref.at[mine], x_s.at[1], x_r.at[1], near_dev))
-    y_in = [go(remote(x_ref, xf_ref.at[mine], y_s.at[0], y_r.at[0], y_dev))]
-    c_in = [go(remote(x_ref, xf_ref.at[mine], c_s.at[0], c_r.at[0], c_dev))]
-    l_in = [go(remote(l_ref, lf_ref.at[mine], l_s.at[o], l_r.at[o], peers[o])) for o in range(1, n)]
-    w_in = [None] * n_z
-    for s in (2, 1, 3):
-        src = w_ref.at[pl.ds(pl.multiple_of(dp * half, 8), half), w_cols(lax.rem(zi + s, n_z))]
-        w_in[s] = go(remote(src, w_half(zi, dp), w_s.at[s], w_r.at[s], (dp, lax.rem(zi + s, n_z), tp)))
-    load_x.wait()
-    load_w.wait()
-    load_l.wait()
-    store_x = pltpu.make_async_copy(x_buf, xf_ref.at[mine], loc.at[0])
-    store_w = pltpu.make_async_copy(w_buf, wf_ref.at[pl.ds(pl.multiple_of(zi * w_rows, 8), w_rows), :], loc.at[1])
-    store_l = pltpu.make_async_copy(l_buf, lf_ref.at[mine], loc.at[2])
-    store_x.start()
-    store_w.start()
-    store_l.start()
-    wx_in = []
-    for j in (2, 1, 3):
+    l_in = [remote(l_ref, lv.at[mine], l_s.at[o], l_r.at[o], peers[o]) for o in range(1, n)]
+    w_in = [None] + [
+        remote(w_ref.at[pl.ds(pl.multiple_of(dp * half, 8), half), w_cols(z_owner[k])], w_half(zi, dp),
+               w_s.at[k], w_r.at[k], (dp, z_owner[k], tp))
+        for k in range(1, n_z)
+    ]
+
+    def own(j):
+        return xv.at[tp * n_z + z_owner[j]]
+
+    def partner(j):
+        return xv.at[y_tp * n_z + z_owner[j]]
+
+    x_in = [None, remote(x_ref, xv.at[mine], x_s.at[1], x_r.at[1], near_dev),
+            remote(x_ref, xv.at[mine], x_s.at[2], x_r.at[2], far_dev),
+            remote(own(2), own(2), x_s.at[3], x_r.at[3], near_dev)]
+    y_in = [remote(own(j) if j else x_ref, own(j), y_s.at[j], y_r.at[j], y_dev) for j in range(n_z)]
+    c_in = [remote(own(j) if j else x_ref, own(j), c_s.at[j], c_r.at[j], c_dev) for j in range(n_z)]
+    c_in += [remote(partner(j), partner(j), c_s.at[n_z + j], c_r.at[n_z + j], c_dev) for j in range(n_z)]
+    wx_in = [None] + [
+        remote(w_half(z_owner[k], dp), w_half(z_owner[k], dp), wx_s.at[k], wx_r.at[k], x_dev)
+        for k in range(1, n_z)
+    ]
+
+    def from_x(j):
         x_in[j].wait_recv()
-        blk = xf_ref.at[tp * n_z + z_owner[j]]
         if j == 2:
-            x_in[3] = go(remote(blk, blk, x_s.at[3], x_r.at[3], near_dev))
-        y_in.append(go(remote(blk, blk, y_s.at[j], y_r.at[j], y_dev)))
-        c_in.append(go(remote(blk, blk, c_s.at[j], c_r.at[j], c_dev)))
-        if j == 3:
-            break
-        w_in[j].wait_recv()
-        part = w_half(lax.rem(zi + n_z - j, n_z), dp)
-        wx_in.append(go(remote(part, part, wx_s.at[j], wx_r.at[j], x_dev)))
-    w_in[3].wait_recv()
-    part = w_half(lax.rem(zi + 1, n_z), dp)
-    wx_in.append(go(remote(part, part, wx_s.at[3], wx_r.at[3], x_dev)))
-    for copy, j in zip(y_in, (0, 2, 1, 3)):
+            x_in[3].start()
+        y_in[j].start()
+        c_in[j].start()
+
+    def from_y(j):
+        y_in[j].wait_recv()
+        c_in[n_z + j].start()
+
+    def from_w(k):
+        w_in[k].wait_recv()
+        wx_in[k].start()
+
+    for copy in [y_in[0], c_in[0]] + l_in + [w_in[1], x_in[1], w_in[2], w_in[3], x_in[2]]:
+        copy.start()
+    from_w(1)
+    from_y(0)
+    from_x(1)
+    from_w(2)
+    from_y(1)
+    from_w(3)
+    for copy in l_in:
         copy.wait_recv()
-        blk = xf_ref.at[y_tp * n_z + z_owner[j]]
-        c_in.append(go(remote(blk, blk, c_s.at[n_z + j], c_r.at[n_z + j], c_dev)))
-    for copy in wx_in + c_in + l_in:
+    for copy in (load_x, load_w, load_l):
+        copy.wait()
+    save_l = pltpu.make_async_copy(lv, lo_ref, loc.at[2])
+    save_l.start()
+    for copy in wx_in[1:]:
         copy.wait_recv()
-    for copy in sends:
+    save_w = pltpu.make_async_copy(wv, wo_ref, loc.at[1])
+    save_w.start()
+
+    before = {2: [lambda: from_x(2)], 7: [lambda: from_y(2)], 8: [lambda: from_x(3)], 11: [lambda: from_y(3)]}
+    for j in range(n_z):
+        before.setdefault(4 * j + 1, []).append(c_in[j].wait_recv)
+        before.setdefault(4 * j + 3, []).append(c_in[n_z + j].wait_recv)
+
+    first_col = tp * vocab_dev + zi * vp
+    valid = lax.min(vocab_dev - zi * vp, vp)
+
+    def outs(slot, block):
+        return (pltpu.make_async_copy(zb.at[slot], zo_ref.at[block], z_sem.at[slot]),
+                pltpu.make_async_copy(xtb.at[slot], xto_ref.at[:, pl.ds(pl.multiple_of(block * rows, LANES), rows)], xt_sem.at[slot]))
+
+    def body(it, carry):
+        owner = flip(zi, it // 2)
+        for slot in range(2):
+            for i in range(slot, n, 2):
+                if i in before:
+                    @pl.when(it == i // 2)
+                    def _():
+                        for act in before[i]:
+                            act()
+            block = flip(tp, lax.rem(it, 2) * 2 + slot) * n_z + owner
+
+            @pl.when(it > 0)
+            def _():
+                for copy in outs(slot, block):
+                    copy.wait()
+
+            lab = lv[block] - first_col
+            lab = jnp.where((lab >= 0) & (lab < valid), lab, -1 - 2 * LANES)
+            st_ref[block] = _logits_block(xv[block], wv, lab, valid, zb.at[slot], xtb.at[slot],
+                                          ms.at[slot], ss.at[slot], ts.at[slot], ls.at[slot])
+            for copy in outs(slot, block):
+                copy.start()
+        return carry
+
+    lax.fori_loop(0, n // 2, body, 0)
+    for slot in range(2):
+        for copy in outs(slot, mine):
+            copy.wait()
+    for copy in l_in + w_in[1:] + x_in[1:] + y_in + c_in + wx_in[1:]:
         copy.wait_send()
-    store_x.wait()
-    store_w.wait()
-    store_l.wait()
-
-
-def _gather_call(w_pad, hidden, labels, vp, n_blocks):
-    w_rows = w_pad.shape[0]
+    save_w.wait()
+    save_l.wait()
+
+
+def _front_call(w_pad, hidden, labels, vp, vocab_dev, n_blocks):
     rows, hid = hidden.shape
+    tokens = n_blocks * rows
     dma = pltpu.SemaphoreType.DMA
+    hbm = pl.BlockSpec(memory_space=pl.ANY)
     return pl.pallas_call(
-        _gather_kernel,
-        in_specs=[pl.BlockSpec(memory_space=pl.ANY)] * 3,
-        out_specs=[pl.BlockSpec(memory_space=pl.ANY)] * 3,
+        functools.partial(_front_kernel, vocab_dev),
+        in_specs=[hbm] * 3,
+        out_specs=[hbm] * 4 + [pl.BlockSpec(memory_space=pltpu.VMEM)],
         out_shape=[
             jax.ShapeDtypeStruct((hid, vp), jnp.bfloat16),
-            jax.ShapeDtypeStruct((n_blocks, rows, hid), jnp.bfloat16),
             jax.ShapeDtypeStruct((n_blocks,) + labels.shape, jnp.int32),
+            jax.ShapeDtypeStruct((n_blocks, rows, vp), jnp.float32),
+            jax.ShapeDtypeStruct((hid, tokens), jnp.bfloat16),
+            jax.ShapeDtypeStruct((n_blocks, STATS, rows), jnp.float32),
         ],
         scratch_shapes=[
-            pltpu.VMEM((w_rows, vp), jnp.bfloat16),
-            pltpu.VMEM((rows, hid), jnp.bfloat16),
-            pltpu.VMEM(labels.shape, jnp.int32),
-            dma((3,)),
+            pltpu.VMEM((hid, vp), jnp.bfloat16),
+            pltpu.VMEM((n_blocks, rows, hid), jnp.bfloat16),
+            pltpu.VMEM((n_blocks,) + labels.shape, jnp.int32),
+            pltpu.VMEM((2, rows, vp), jnp.float32),
+            pltpu.VMEM((2, hid, rows), jnp.bfloat16),
+        ] + [pltpu.VMEM((2, rows, LANES), jnp.float32)] * 3 + [
+            pltpu.VMEM((2, rows, LANES), jnp.int32),
+            dma((3,)), dma((2,)), dma((2,)),
         ] + [dma((4,))] * 8 + [dma((8,))] * 2 + [dma((16,))] * 2,
         compiler_params=pltpu.CompilerParams(collective_id=0, has_side_effects=True, vmem_limit_bytes=VMEM_LIMIT),
-        name="gather",
+        name="front",
     )(w_pad, hidden, labels)
 
 
@@ -307,36 +369,6 @@
     )(st)
 
 
-def _logits_call(x_all, w, lab, valid):
-    n_blocks, rows, hid = x_all.shape
-    vp = w.shape[1]
-    tokens = n_blocks * rows
-    return pl.pallas_call(
-        functools.partial(_logits_kernel, vp),
-        grid=(n_blocks,),
-        in_specs=[
-            pl.BlockSpec(memory_space=pltpu.SMEM),
-            pl.BlockSpec((1, rows, hid), lambda i: (i, 0, 0)),
-            pl.BlockSpec((hid, vp), lambda i: (0, 0)),
-            pl.BlockSpec((1, 8, rows), lambda i: (i, 0, 0)),
-        ],
-        out_specs=[
-            pl.BlockSpec((1, rows, vp), lambda i: (i, 0, 0)),
-            pl.BlockSpec((1, STATS, rows), lambda i: (i, 0, 0)),
-            pl.BlockSpec((hid, rows), lambda i: (0, i)),
-        ],
-        out_shape=[
-            jax.ShapeDtypeStruct((n_blocks, rows, vp), jnp.float32),
-            jax.ShapeDtypeStruct((n_blocks, STATS, rows), jnp.float32),
-            jax.ShapeDtypeStruct((hid, tokens), jnp.bfloat16),
-        ],
-        scratch_shapes=[pltpu.VMEM((rows, LANES), jnp.float32)] * 3 + [pltpu.VMEM((rows, LANES), jnp.int32)],
-        compiler_params=pltpu.CompilerParams(vmem_limit_bytes=VMEM_LIMIT),
-        cost_estimate=pl.CostEstimate(flops=2 * tokens * hid * vp, bytes_accessed=tokens * vp * 4, transcendentals=tokens * vp),
-        name="logits_stats",
-    )(valid, x_all, w, lab)
-
-
 def _grad_call(c, ids, z, w, st, lab, g_all, v0, sub):
     n_blocks, rows, vp = z.shape
     hid = w.shape[0]
@@ -464,14 +496,13 @@
         yi, ci = tpi // 2, tpi % 2
 
         w_pad = jnp.pad(w_head, ((0, 0), (0, n_z * vp - vocab_dev)))
-        w_full, x_all, lab = _gather_call(w_pad, hidden, labels.reshape(1, rows_dev), vp, n_blocks)
+        w_full, lab, z_all, xt, local = _front_call(w_pad, hidden, labels.reshape(1, rows_dev), vp, vocab_dev, n_blocks)
 
         lab = lab - (tpi * vocab_dev + zi * vp)
         valid = jnp.minimum(vocab_dev - zi * vp, vp).astype(jnp.int32)
         lab = jnp.where((lab >= 0) & (lab < valid), lab, -1 - 2 * LANES).astype(jnp.float32)
         lab = jnp.broadcast_to(lab, (n_blocks, 8, rows_dev))
 
-        z_all, local, xt = _logits_call(x_all, w_full, lab, valid.reshape(1))
         st = _stats_call(local)
         mean_loss = (jnp.sum(st[:, 2]) * (1.0 / tokens)).reshape(1)
 
@@ -514,17 +545,36 @@
                 sent.append(z_shift(parts[s], s))
             return parts, sent
 
+        def wide_near(c, *deps):
+            both = (_after(keeps[c], *deps) + gots[c]).reshape(2, 2, 2, sub, hid)
+            odd = zi % 2
+            mine, other = pick(both, odd, 2), pick(both, 1 - odd, 2)
+            nears[c] = (mine, swap(other, "fsdp", 1))
+            return mine, other
+
+        def wide_far(c, *deps):
+            both = _after(nears[c][0], *deps) + nears[c][1]
+            high = zi // 2
+            mine, other = pick(both, high, 1), pick(both, 1 - high, 1)
+            fars[c] = (mine, swap(other, "fsdp", 2))
+            return mine, other
+
+        def wide_y(c, *deps):
+            both = _after(fars[c][0], *deps) + fars[c][1]
+            fars[c] = (both[0], swap(both[1], "tp", 2))
+            return (both,)
+
         keeps, gots, ys, nears, fars = ([None] * CHUNKS for _ in range(5))
         g, keeps[0], gots[0] = grad(0, None)
         g, keeps[1], gots[1] = grad(1, g, keeps[0])
-        t = to_y(0, keeps[1])
+        t = wide_near(0, keeps[1])
         g, keeps[2], gots[2] = grad(2, g, *t)
         t = to_y(1, keeps[2])
         g, keeps[3], gots[3] = grad(3, g, *t)
-        t = to_y(2, keeps[3]) + to_near(0, keeps[3])
+        t = to_y(2, keeps[3]) + wide_far(0, keeps[3])
         dw0 = _dw_call(_after(xt, *t), g[0]).reshape(n_z, w_rows, v0)
         parts0, pieces0 = send_dw(dw0)
-        t = to_y(3, dw0) + to_near(1, dw0) + to_far(0, dw0) + tuple(parts0)
+        t = to_near(1, dw0) + to_y(3, dw0) + wide_y(0, dw0) + tuple(parts0)
         dw1 = _dw_call(_after(xt, *t), g[1]).reshape(n_z, w_rows, vp - v0)
         parts1, pieces1 = send_dw(dw1)
         t = to_near(2, *parts1)

time: 605 us -> 580 us (0.959)
  Pallas kernels: 350 us -> 335 us
  waiting for transfers between devices: 144 us -> 134 us
    pallas_call x2 -> x1, Pallas kernels: 185 us -> 170 us  [_front_call(): pl.pallas_call(functools.partial(_front_kernel, vocab_dev), in_specs=[hbm...]
    ppermute x16, waiting for transfers between devices: 121 us -> 110 us  [swap(): lax.ppermute(a, axis, [(k, k ^ bit) for k in range(mesh.shape[axis])])]
    add x4 -> x3, other arithmetic: 15.8 us -> 11.5 us  [to_y(): other = keep[1] + gots[c][1]]
  transfers between devices with their start and end apart: 22 -> 22, of which waited for: 6 -> 6; matrix products, arithmetic and copies ran while one was open for 7% -> 7% of each run, Pallas kernels for 21% -> 22%
where the time goes in v2:
time: 580 us; the launch traced here: 570 us
  Pallas kernels  335 us (58%)
  waiting for transfers between devices  134 us (23%)
  starting transfers between devices  47.8 us (8%)
  other arithmetic  29.9 us (5%)
  local copies, waits for them, and re-layouts  20.5 us (4%)
    pallas_call x1, Pallas kernels, _front_call(): pl.pallas_call(functools.partial(_front_kernel, vocab_dev), in_specs=[hbm...  170 us
    ppermute x16, waiting for transfers between devices, swap(): lax.ppermute(a, axis, [(k, k ^ bit) for k in range(mesh.shape[axis])])  110 us
    pallas_call x4, Pallas kernels, _grad_call(): pl.pallas_call(functools.partial(_grad_kernel, v0, 1.0 / tokens), grid_sp...  92.3 us
    pallas_call x2, Pallas kernels, _dw_call(): pl.pallas_call(functools.partial(_dw_kernel, steps), grid=(steps,), in_sp...  54 us
    ppermute x6, starting transfers between devices, z_shift(): return lax.ppermute(a, 'fsdp', [(k, (k + s) % n_z) for k in range(n_z)])  32.2 us
    ppermute x6, waiting for transfers between devices, z_shift(): return lax.ppermute(a, 'fsdp', [(k, (k + s) % n_z) for k in range(n_z)])  23.5 us
    ppermute x16, starting transfers between devices, swap(): lax.ppermute(a, axis, [(k, k ^ bit) for k in range(mesh.shape[axis])])  15.6 us
    pallas_call x1, Pallas kernels, _stats_call(): pl.pallas_call(_stats_kernel, in_specs=[vmem], out_specs=vmem, out_shape=...  14.1 us
  transfers between devices with their start and end apart: 22, of which 6 were waited for; matrix products, arithmetic and copies ran while one was open for 7% of the time, Pallas kernels for 22%

profile of v2, /device:TPU:0, one launch (start us, length us, event | category | flops | bytes accessed | tf_op | source)
XLA Modules:
  0.0 569.5 jit_solution(8258008433444282552)
XLA Ops:
  0.7 5.0 pad.4.w_ref
  5.6 169.5 %front.1 = (bf16[768,3200]{1,0:T(8,128)(2,1)}, s32[16,1,512]{2,1,0:T(1,128)}, f32[16,512,3200]{2,1,0:T(8,128)}, bf16[768,8192]{1,0:T(8,128)(2,1)}, f32[16,4,512]{2,1,0:T(4,128)}) custom-call(bf16[192,12800]{1,0:T(8,128)(2,1)} %pad.4.w_ref, bf16[512,768]{1,0:T(8,128)(2,1)} %x_ref.1, s32[1,512]{1,0:T(1,128)} %bitcast.89), custom_call_target="tpu_custom_call" | custom-call | tf_op jit(solution)/shard_map/front/pallas_call | solution.py:287
  176.0 14.1 %stats.1.st_ref = f32[16,4,512]{2,1,0:T(4,128)} custom-call(f32[16,4,512]{2,1,0:T(4,128)} %get-tuple-element.46.st_ref), custom_call_target="tpu_custom_call" | custom-call | tf_op jit(solution)/shard_map/stats/pallas_call | solution.py:361
  191.4 23.0 %grad_dx.4 = (bf16[16,512,1536]{2,1,0:T(8,128)(2,1)}, bf16[16,512,1664]{2,1,0:T(8,128)(2,1)}, f32[2,4,128,768]{3,2,1,0:T(8,128)}, f32[2,4,128,768]{3,2,1,0:T(8,128)}) custom-call(s32[2]{0:T(128)} %pad_add_fusion.ids_ref, f32[16,512,3200]{2,1,0:T(8,128)} %get-tuple-element.47.z_ref, bf16[768,3200]{1,0:T(8,128)(2,1)} %get-tuple-element.48.w_ref, ...), custom_call_target="tpu_custom_call" | custom-call | flops 10066329600 | bytes 39321600 | tf_op jit(solution)/shard_map/grad_dx/pallas_call | solution.py:390
  214.5 23.3 %grad_dx.5 = (bf16[16,512,1536]{2,1,0:T(8,128)(2,1)}, bf16[16,512,1664]{2,1,0:T(8,128)(2,1)}, f32[2,4,128,768]{3,2,1,0:T(8,128)}, f32[2,4,128,768]{3,2,1,0:T(8,128)}) custom-call(s32[2]{0:T(128)} %pad_add_fusion.ids_ref, f32[16,512,3200]{2,1,0:T(8,128)} %get-tuple-element.47.z_ref, ...), custom_call_target="tpu_custom_call", output_to_operand_aliasing={{0}: (5, {}), {1}: (6, {})} | custom-call | flops 10066329600 | bytes 39321600 | tf_op jit(solution)/shard_map/grad_dx/pallas_call | solution.py:390
  238.2 2.3 add.169
  242.0 23.0 %grad_dx.6 = (bf16[16,512,1536]{2,1,0:T(8,128)(2,1)}, bf16[16,512,1664]{2,1,0:T(8,128)(2,1)}, f32[2,4,128,768]{3,2,1,0:T(8,128)}, f32[2,4,128,768]{3,2,1,0:T(8,128)}) custom-call(s32[2]{0:T(128)} %pad_add_fusion.ids_ref, f32[16,512,3200]{2,1,0:T(8,128)} %get-tuple-element.47.z_ref, ...), custom_call_target="tpu_custom_call", output_to_operand_aliasing={{0}: (5, {}), {1}: (6, {})} | custom-call | flops 10066329600 | bytes 39321600 | tf_op jit(solution)/shard_map/grad_dx/pallas_call | solution.py:390
  265.7 4.4 fusion.4
  270.2 23.0 %grad_dx.7 = (bf16[16,512,1536]{2,1,0:T(8,128)(2,1)}, bf16[16,512,1664]{2,1,0:T(8,128)(2,1)}, f32[2,4,128,768]{3,2,1,0:T(8,128)}, f32[2,4,128,768]{3,2,1,0:T(8,128)}) custom-call(s32[2]{0:T(128)} %pad_add_fusion.ids_ref, f32[16,512,3200]{2,1,0:T(8,128)} %get-tuple-element.47.z_ref, ...), custom_call_target="tpu_custom_call", output_to_operand_aliasing={{0}: (5, {}), {1}: (6, {})} | custom-call | flops 10066329600 | bytes 39321600 | tf_op jit(solution)/shard_map/grad_dx/pallas_call | solution.py:390
  294.3 7.8 %collective-permute-done.2 = f32[2,2,128,768]{3,2,1,0:T(8,128)} collective-permute-done((f32[2,2,128,768]{3,2,1,0:T(8,128)}, f32[2,2,128,768]{3,2,1,0:T(8,128)}, u32[]{:S(2)}, u32[]{:S(2)}) %collective-permute-start.2) | collective-permute-done | bytes 1572896 | tf_op jit(solution)/shard_map/ppermute | solution.py:483
  306.2 3.5 fusion.2
  309.6 25.2 %dw.2 = bf16[768,1536]{1,0:T(8,128)(2,1)} custom-call(bf16[768,8192]{1,0:T(8,128)(2,1)} %get-tuple-element.77.xt_ref, bf16[16,512,1536]{2,1,0:T(8,128)(2,1)} %get-tuple-element.72.g_ref), custom_call_target="tpu_custom_call" | custom-call | flops 19327352832 | bytes 37748736 | tf_op jit(solution)/shard_map/dw/pallas_call | solution.py:426
  340.6 3.6 fusion
  348.3 28.7 %dw.3 = bf16[768,1664]{1,0:T(8,128)(2,1)} custom-call(bf16[768,8192]{1,0:T(8,128)(2,1)} %get-tuple-element.77.xt_ref, bf16[16,512,1664]{2,1,0:T(8,128)(2,1)} %get-tuple-element.78.g_ref), custom_call_target="tpu_custom_call" | custom-call | flops 20937965568 | bytes 39845888 | tf_op jit(solution)/shard_map/dw/pallas_call | solution.py:426
  377.0 3.2 dynamic-slice_bitcast_fusion.10
  386.1 18.6 %collective-permute-done.9 = f32[4,128,768]{2,1,0:T(8,128)} collective-permute-done((f32[4,128,768]{2,1,0:T(8,128)}, f32[4,128,768]{2,1,0:T(8,128)}, u32[]{:S(2)}, u32[]{:S(2)}) %collective-permute-start.9) | collective-permute-done | bytes 1572896 | tf_op jit(solution)/shard_map/ppermute | solution.py:483
  414.9 2.4 collective-permute-start.13
  417.5 43.1 %collective-permute-done.11 = f32[2,128,768]{2,1,0:T(8,128)} collective-permute-done((f32[2,128,768]{2,1,0:T(8,128)}, f32[2,128,768]{2,1,0:T(8,128)}, u32[]{:S(2)}, u32[]{:S(2)}) %collective-permute-start.11) | collective-permute-done | bytes 786464 | tf_op jit(solution)/shard_map/ppermute | solution.py:483
  461.9 3.0 collective-permute-start.15
  468.0 32.2 %collective-permute-done.14 = f32[128,768]{1,0:T(8,128)S(1)} collective-permute-done((f32[128,768]{1,0:T(8,128)S(1)}, f32[128,768]{1,0:T(8,128)S(1)}, u32[]{:S(2)}, u32[]{:S(2)}) %collective-permute-start.14) | collective-permute-done | bytes 393248 | tf_op jit(solution)/shard_map/ppermute | solution.py:483
  500.2 8.4 %collective-permute-done.15 = f32[128,768]{1,0:T(8,128)S(1)} collective-permute-done((f32[128,768]{1,0:T(8,128)S(1)}, f32[128,768]{1,0:T(8,128)S(1)}, u32[]{:S(2)}, u32[]{:S(2)}) %collective-permute-start.15) | collective-permute-done | bytes 393248 | tf_op jit(solution)/shard_map/ppermute | solution.py:483
  508.6 28.2 %collective-permute-start.20 = (bf16[192,1536]{1,0:T(8,128)(2,1)S(1)}, bf16[192,1536]{1,0:T(8,128)(2,1)S(1)}, u32[]{:S(2)}, u32[]{:S(2)}) collective-permute-start(bf16[192,1536]{1,0:T(8,128)(2,1)S(1)} %copy-done.13), channel_id=1, source_target_pairs={{0,12},{4,0},{8,4},{12,8},{1,13},{5,1},{9,5},{13,9},{2,14},{6,2},{... | collective-permute-start | bytes 1769480 | tf_op jit(solution)/shard_map/ppermute | solution.py:480
  537.8 23.5 %collective-permute-done.18.refs_4_ = bf16[192,1536]{1,0:T(8,128)(2,1)S(1)} collective-permute-done((bf16[192,1536]{1,0:T(8,128)(2,1)S(1)}, bf16[192,1536]{1,0:T(8,128)(2,1)S(1)}, u32[]{:S(2)}, u32[]{:S(2)}) %collective-permute-start.18) | collective-permute-done | bytes 589856 | tf_op jit(solution)/shard_map/ppermute | solution.py:480
  563.4 5.0 place.1
  (93 shorter events, 42.8 us)
Async XLA Ops:
  214.5 23.7 %collective-permute-start = (f32[2,4,128,768]{3,2,1,0:T(8,128)}, f32[2,4,128,768]{3,2,1,0:T(8,128)}, u32[]{:S(2)}, u32[]{:S(2)}) collective-permute-start(f32[2,4,128,768]{3,2,1,0:T(8,128)} %get-tuple-element.56), channel_id=1, source_target_pairs={{0,1},{1,0},{2,3},{3,2},{4,5},{5,4},{6,7},{7,6},{8,9},{9,8},{10,11... | collective-permute-start | bytes 9437192 | tf_op jit(solution)/shard_map/ppermute | solution.py:483
  237.8 27.9 %collective-permute-start.1 = (f32[2,4,128,768]{3,2,1,0:T(8,128)}, f32[2,4,128,768]{3,2,1,0:T(8,128)}, u32[]{:S(2)}, u32[]{:S(2)}) collective-permute-start(f32[2,4,128,768]{3,2,1,0:T(8,128)} %get-tuple-element.62), channel_id=1, source_target_pairs={{0,1},{1,0},{2,3},{3,2},{4,5},{5,4},{6,7},{7,6},{8,9},{9,8},{10,11... | collective-permute-start | bytes 9437192 | tf_op jit(solution)/shard_map/ppermute | solution.py:483
  265.0 41.0 %collective-permute-start.3 = (f32[2,4,128,768]{3,2,1,0:T(8,128)}, f32[2,4,128,768]{3,2,1,0:T(8,128)}, u32[]{:S(2)}, u32[]{:S(2)}) collective-permute-start(f32[2,4,128,768]{3,2,1,0:T(8,128)} %get-tuple-element.70), channel_id=1, source_target_pairs={{0,1},{1,0},{2,3},{3,2},{4,5},{5,4},{6,7},{7,6},{8,9},{9,8},{10,11... | collective-permute-start | bytes 9437192 | tf_op jit(solution)/shard_map/ppermute | solution.py:483
  265.1 37.0 %collective-permute-start.2 = (f32[2,2,128,768]{3,2,1,0:T(8,128)}, f32[2,2,128,768]{3,2,1,0:T(8,128)}, u32[]{:S(2)}, u32[]{:S(2)}) collective-permute-start(f32[2,2,128,768]{3,2,1,0:T(8,128)} %get-tuple-element.95), channel_id=1, source_target_pairs={{0,4},{4,0},{8,12},{12,8},{1,5},{5,1},{9,13},{13,9},{2,6},{6,2},{1... | collective-permute-start | bytes 4718600 | tf_op jit(solution)/shard_map/ppermute | solution.py:483
  293.1 47.4 %collective-permute-start.5 = (f32[2,4,128,768]{3,2,1,0:T(8,128)}, f32[2,4,128,768]{3,2,1,0:T(8,128)}, u32[]{:S(2)}, u32[]{:S(2)}) collective-permute-start(f32[2,4,128,768]{3,2,1,0:T(8,128)} %get-tuple-element.75), channel_id=1, source_target_pairs={{0,1},{1,0},{2,3},{3,2},{4,5},{5,4},{6,7},{7,6},{8,9},{9,8},{10,11... | collective-permute-start | bytes 9437192 | tf_op jit(solution)/shard_map/ppermute | solution.py:483
  293.2 42.9 %collective-permute-start.6 = (f32[4,128,768]{2,1,0:T(8,128)}, f32[4,128,768]{2,1,0:T(8,128)}, u32[]{:S(2)}, u32[]{:S(2)}) collective-permute-start(f32[4,128,768]{2,1,0:T(8,128)} %get-tuple-element.93), channel_id=1, source_target_pairs={{0,2},{1,3},{2,0},{3,1},{4,6},{5,7},{6,4},{7,5},{8,10},{9,11},{10,... | collective-permute-start | bytes 4718600 | tf_op jit(solution)/shard_map/ppermute | solution.py:483
  305.0 41.1 %collective-permute-start.4 = (f32[2,128,768]{2,1,0:T(8,128)}, f32[2,128,768]{2,1,0:T(8,128)}, u32[]{:S(2)}, u32[]{:S(2)}) collective-permute-start(f32[2,128,768]{2,1,0:T(8,128)} %get-tuple-element.111), channel_id=1, source_target_pairs={{0,8},{4,12},{8,0},{12,4},{1,9},{5,13},{9,1},{13,5},{2,10},{6,14},... | collective-permute-start | bytes 2359304 | tf_op jit(solution)/shard_map/ppermute | solution.py:483
  334.9 45.4 %collective-permute-start.7 = (f32[4,128,768]{2,1,0:T(8,128)}, f32[4,128,768]{2,1,0:T(8,128)}, u32[]{:S(2)}, u32[]{:S(2)}) collective-permute-start(f32[4,128,768]{2,1,0:T(8,128)} %get-tuple-element.91), channel_id=1, source_target_pairs={{0,2},{1,3},{2,0},{3,1},{4,6},{5,7},{6,4},{7,5},{8,10},{9,11},{10,... | collective-permute-start | bytes 4718600 | tf_op jit(solution)/shard_map/ppermute | solution.py:483
  339.0 45.0 %collective-permute-start.8 = (f32[2,128,768]{2,1,0:T(8,128)}, f32[2,128,768]{2,1,0:T(8,128)}, u32[]{:S(2)}, u32[]{:S(2)}) collective-permute-start(f32[2,128,768]{2,1,0:T(8,128)} %get-tuple-element.109), channel_id=1, source_target_pairs={{0,4},{4,0},{8,12},{12,8},{1,5},{5,1},{9,13},{13,9},{2,6},{6,2},{1... | collective-permute-start | bytes 2359304 | tf_op jit(solution)/shard_map/ppermute | solution.py:483
  344.1 60.6 %collective-permute-start.9 = (f32[4,128,768]{2,1,0:T(8,128)}, f32[4,128,768]{2,1,0:T(8,128)}, u32[]{:S(2)}, u32[]{:S(2)}) collective-permute-start(f32[4,128,768]{2,1,0:T(8,128)} %get-tuple-element.89), channel_id=1, source_target_pairs={{0,2},{1,3},{2,0},{3,1},{4,6},{5,7},{6,4},{7,5},{8,10},{9,11},{10,... | collective-permute-start | bytes 4718600 | tf_op jit(solution)/shard_map/ppermute | solution.py:483
  382.9 32.1 %collective-permute-start.10 = (f32[2,128,768]{2,1,0:T(8,128)}, f32[2,128,768]{2,1,0:T(8,128)S(1)}, u32[]{:S(2)}, u32[]{:S(2)}) collective-permute-start(f32[2,128,768]{2,1,0:T(8,128)} %get-tuple-element.107), channel_id=1, source_target_pairs={{0,4},{4,0},{8,12},{12,8},{1,5},{5,1},{9,13},{13,9},{2,6},{6,2},{1... | collective-permute-start | bytes 2359304 | tf_op jit(solution)/shard_map/ppermute | solution.py:483
  407.4 53.2 %collective-permute-start.11 = (f32[2,128,768]{2,1,0:T(8,128)}, f32[2,128,768]{2,1,0:T(8,128)}, u32[]{:S(2)}, u32[]{:S(2)}) collective-permute-start(f32[2,128,768]{2,1,0:T(8,128)} %get-tuple-element.105), channel_id=1, source_target_pairs={{0,4},{4,0},{8,12},{12,8},{1,5},{5,1},{9,13},{13,9},{2,6},{6,2},{1... | collective-permute-start | bytes 2359304 | tf_op jit(solution)/shard_map/ppermute | solution.py:483
  409.1 52.8 %collective-permute-start.12 = (f32[128,768]{1,0:T(8,128)}, f32[128,768]{1,0:T(8,128)}, u32[]{:S(2)}, u32[]{:S(2)}) collective-permute-start(f32[128,768]{1,0:T(8,128)} %get-tuple-element.113), channel_id=1, source_target_pairs={{0,2},{1,3},{2,0},{3,1},{4,6},{5,7},{6,4},{7,5},{8,10},{9,11},{10,... | collective-permute-start | bytes 1179656 | tf_op jit(solution)/shard_map/ppermute | solution.py:483
  410.7 55.3 %collective-permute-start.16 = (bf16[192,1536]{1,0:T(8,128)(2,1)}, bf16[192,1536]{1,0:T(8,128)(2,1)}, u32[]{:S(2)}, u32[]{:S(2)}) collective-permute-start(bf16[192,1536]{1,0:T(8,128)(2,1)} %get-tuple-element.103), channel_id=1, source_target_pairs={{0,4},{4,8},{8,12},{12,0},{1,5},{5,9},{9,13},{13,1},{2,6},{6,10},{... | collective-permute-start | bytes 1769480 | tf_op jit(solution)/shard_map/ppermute | solution.py:480
  413.4 147.8 %collective-permute-start.17 = (bf16[192,1664]{1,0:T(8,128)(2,1)}, bf16[192,1664]{1,0:T(8,128)(2,1)}, u32[]{:S(2)}, u32[]{:S(2)}) collective-permute-start(bf16[192,1664]{1,0:T(8,128)(2,1)} %get-tuple-element.99), channel_id=1, source_target_pairs={{0,4},{4,8},{8,12},{12,0},{1,5},{5,9},{9,13},{13,1},{2,6},{6,10},{... | collective-permute-start | bytes 1916936 | tf_op jit(solution)/shard_map/ppermute | solution.py:480
  414.9 51.2 %collective-permute-start.13 = (f32[128,768]{1,0:T(8,128)}, f32[128,768]{1,0:T(8,128)S(1)}, u32[]{:S(2)}, u32[]{:S(2)}) collective-permute-start(f32[128,768]{1,0:T(8,128)} %get-tuple-element.119), channel_id=1, source_target_pairs={{0,8},{4,12},{8,0},{12,4},{1,9},{5,13},{9,1},{13,5},{2,10},{6,14},... | collective-permute-start | bytes 1179656 | tf_op jit(solution)/shard_map/ppermute | solution.py:483
  460.6 39.6 %collective-permute-start.14 = (f32[128,768]{1,0:T(8,128)S(1)}, f32[128,768]{1,0:T(8,128)S(1)}, u32[]{:S(2)}, u32[]{:S(2)}) collective-permute-start(f32[128,768]{1,0:T(8,128)S(1)} %get-tuple-element.117), channel_id=1, source_target_pairs={{0,8},{4,12},{8,0},{12,4},{1,9},{5,13},{9,1},{13,5},{2,10},{6,14},... | collective-permute-start | bytes 1179656 | tf_op jit(solution)/shard_map/ppermute | solution.py:483
  461.8 38.4 %copy-start.14 = (bf16[192,1536]{1,0:T(8,128)(2,1)S(1)}, bf16[192,1536]{1,0:T(8,128)(2,1)}, u32[]{:S(2)}) copy-start(bf16[192,1536]{1,0:T(8,128)(2,1)} %get-tuple-element.102) | copy-start | bytes 1769476
  461.8 46.8 %copy-start.13 = (bf16[192,1536]{1,0:T(8,128)(2,1)S(1)}, bf16[192,1536]{1,0:T(8,128)(2,1)}, u32[]{:S(2)}) copy-start(bf16[192,1536]{1,0:T(8,128)(2,1)} %get-tuple-element.101) | copy-start | bytes 1769476
  461.9 46.7 %collective-permute-start.15 = (f32[128,768]{1,0:T(8,128)S(1)}, f32[128,768]{1,0:T(8,128)S(1)}, u32[]{:S(2)}, u32[]{:S(2)}) collective-permute-start(f32[128,768]{1,0:T(8,128)S(1)} %get-tuple-element.115), channel_id=1, source_target_pairs={{0,8},{4,12},{8,0},{12,4},{1,9},{5,13},{9,1},{13,5},{2,10},{6,14},... | collective-permute-start | bytes 1179656 | tf_op jit(solution)/shard_map/ppermute | solution.py:483
  465.9 95.3 %collective-permute-start.19 = (bf16[192,1664]{1,0:T(8,128)(2,1)S(1)}, bf16[192,1664]{1,0:T(8,128)(2,1)S(1)}, u32[]{:S(2)}, u32[]{:S(2)}) collective-permute-start(bf16[192,1664]{1,0:T(8,128)(2,1)S(1)} %copy-done.10), channel_id=1, source_target_pairs={{0,8},{4,12},{8,0},{12,4},{1,9},{5,13},{9,1},{13,5},{2,10},{6,14},... | collective-permute-start | bytes 1916936 | tf_op jit(solution)/shard_map/ppermute | solution.py:480
  466.2 95.1 %collective-permute-start.21 = (bf16[192,1664]{1,0:T(8,128)(2,1)S(1)}, bf16[192,1664]{1,0:T(8,128)(2,1)S(1)}, u32[]{:S(2)}, u32[]{:S(2)}) collective-permute-start(bf16[192,1664]{1,0:T(8,128)(2,1)S(1)} %copy-done.9), channel_id=1, source_target_pairs={{0,12},{4,0},{8,4},{12,8},{1,13},{5,1},{9,5},{13,9},{2,14},{6,2},{... | collective-permute-start | bytes 1916936 | tf_op jit(solution)/shard_map/ppermute | solution.py:480
  500.2 61.1 %collective-permute-start.18 = (bf16[192,1536]{1,0:T(8,128)(2,1)S(1)}, bf16[192,1536]{1,0:T(8,128)(2,1)S(1)}, u32[]{:S(2)}, u32[]{:S(2)}) collective-permute-start(bf16[192,1536]{1,0:T(8,128)(2,1)S(1)} %copy-done.14), channel_id=1, source_target_pairs={{0,8},{4,12},{8,0},{12,4},{1,9},{5,13},{9,1},{13,5},{2,10},{6,14},... | collective-permute-start | bytes 1769480 | tf_op jit(solution)/shard_map/ppermute | solution.py:480
  508.6 52.7 %collective-permute-start.20 = (bf16[192,1536]{1,0:T(8,128)(2,1)S(1)}, bf16[192,1536]{1,0:T(8,128)(2,1)S(1)}, u32[]{:S(2)}, u32[]{:S(2)}) collective-permute-start(bf16[192,1536]{1,0:T(8,128)(2,1)S(1)} %copy-done.13), channel_id=1, source_target_pairs={{0,12},{4,0},{8,4},{12,8},{1,13},{5,1},{9,5},{13,9},{2,14},{6,2},{... | collective-permute-start | bytes 1769480 | tf_op jit(solution)/shard_map/ppermute | solution.py:480
  (13 other events, 51.9 us)

commit v3 on v2

--- a/solution.py
+++ b/solution.py
@@ -418,9 +418,9 @@
     )(ids, z, w, st, lab, *extra)
 
 
-def _dw_call(xt, g):
+def _dw_call(xt, g, width, col=0):
     hid, tokens = xt.shape
-    sub, width = g.shape[1:]
+    sub = g.shape[1]
     kb = 1024
     steps = tokens // kb
     return pl.pallas_call(
@@ -428,7 +428,7 @@
         grid=(steps,),
         in_specs=[
             pl.BlockSpec((hid, kb), lambda k: (0, k)),
-            pl.BlockSpec((kb // sub, sub, width), lambda k: (k, 0, 0)),
+            pl.BlockSpec((kb // sub, sub, width), lambda k: (k, 0, col)),
         ],
         out_specs=pl.BlockSpec((hid, width), lambda k: (0, 0)),
         out_shape=jax.ShapeDtypeStruct((hid, width), jnp.bfloat16),
@@ -439,22 +439,25 @@
     )(xt, g)
 
 
-def _place_kernel(n_z, v0, zi_ref, *refs):
+def _place_kernel(n_z, edges, zi_ref, *refs):
     o_ref = refs[-1]
     j = pl.program_id(0)
     dist = lax.rem(zi_ref[0] + n_z - j, n_z)
     for s in range(n_z):
         @pl.when(dist == s)
         def _():
-            o_ref[:, :v0] = refs[2 * s][...]
-            o_ref[:, v0:] = refs[2 * s + 1][...]
-
-
-def _place_call(zi, pieces, vp, vocab_dev):
-    n_z = len(pieces) // 2
-    rows, v0 = pieces[0].shape
+            for m, (c0, c1) in enumerate(edges):
+                o_ref[:, c0:c1] = refs[len(edges) * s + m][...]
+
+
+def _place_call(zi, pieces, n_z, vp, vocab_dev):
+    rows = pieces[0].shape[0]
+    edges, c0 = [], 0
+    for p in pieces[:len(pieces) // n_z]:
+        edges.append((c0, c0 + p.shape[1]))
+        c0 += p.shape[1]
     return pl.pallas_call(
-        functools.partial(_place_kernel, n_z, v0),
+        functools.partial(_place_kernel, n_z, edges),
         grid=(n_z,),
         in_specs=[pl.BlockSpec(memory_space=pltpu.SMEM)]
         + [pl.BlockSpec(p.shape, lambda j: (0, 0)) for p in pieces],
@@ -571,11 +574,15 @@
         g, keeps[2], gots[2] = grad(2, g, *t)
         t = to_y(1, keeps[2])
         g, keeps[3], gots[3] = grad(3, g, *t)
-        t = to_y(2, keeps[3]) + wide_far(0, keeps[3])
-        dw0 = _dw_call(_after(xt, *t), g[0]).reshape(n_z, w_rows, v0)
+        t = to_y(2, keeps[3])
+        vh = v0 // 2
+        dwa = _dw_call(_after(xt, *t), g[0], vh, 0).reshape(n_z, w_rows, vh)
+        partsa, piecesa = send_dw(dwa)
+        t = wide_far(0, dwa) + tuple(partsa)
+        dw0 = _dw_call(_after(xt, *t), g[0], vh, 1).reshape(n_z, w_rows, vh)
         parts0, pieces0 = send_dw(dw0)
         t = to_near(1, dw0) + to_y(3, dw0) + wide_y(0, dw0) + tuple(parts0)
-        dw1 = _dw_call(_after(xt, *t), g[1]).reshape(n_z, w_rows, vp - v0)
+        dw1 = _dw_call(_after(xt, *t), g[1], vp - v0).reshape(n_z, w_rows, vp - v0)
         parts1, pieces1 = send_dw(dw1)
         t = to_near(2, *parts1)
         t = to_far(1, *t)
@@ -583,9 +590,9 @@
         t = to_far(2, *t)
         t = to_far(3, *t)
         out = [last(c, *t) for c in range(CHUNKS)]
-        pieces = [p for pair in zip(pieces0, pieces1) for p in pair]
+        pieces = [p for group in zip(piecesa, pieces0, pieces1) for p in group]
         zv = _after(zi.reshape(1).astype(jnp.int32), *out)
-        d_w = _place_call(zv, pieces, vp, vocab_dev)
+        d_w = _place_call(zv, pieces, n_z, vp, vocab_dev)
         return mean_loss, jnp.concatenate(out, axis=0), d_w
 
     return jax.shard_map(

time: 580 us -> 593 us (1.022); the launches traced: 570 us -> 593 us
  starting transfers between devices: 47.8 us -> 62.9 us
  Pallas kernels: 335 us -> 342 us
    ppermute x6 -> x9, starting transfers between devices: 32.2 us -> 49.5 us  [z_shift(): return lax.ppermute(a, 'fsdp', [(k, (k + s) % n_z) for k in range(n_z)])]
    pallas_call x2 -> x3, Pallas kernels: 54 us -> 61 us  [_dw_call(): pl.pallas_call(functools.partial(_dw_kernel, steps), grid=(steps,), in_sp...]
    ppermute x6 -> x9, waiting for transfers between devices: 23.5 us -> 23.8 us  [z_shift(): return lax.ppermute(a, 'fsdp', [(k, (k + s) % n_z) for k in range(n_z)])]
    squeeze x10 -> x11, local copies, waits for them, and re-layouts: 11.7 us -> 11.9 us  [pick(): return lax.dynamic_index_in_dim(a, i, axis, keepdims=False)]
  transfers between devices with their start and end apart: 22 -> 25, of which waited for: 6 -> 9; matrix products, arithmetic and copies ran while one was open for 7% -> 7% of each run, Pallas kernels for 22% -> 22%
where the time goes in v3:
time: 593 us
  Pallas kernels  342 us (58%)
  waiting for transfers between devices  132 us (22%)
  starting transfers between devices  62.9 us (11%)
  other arithmetic  32.1 us (5%)
  local copies, waits for them, and re-layouts  21.3 us (4%)
    pallas_call x1, Pallas kernels, _front_call(): pl.pallas_call(functools.partial(_front_kernel, vocab_dev), in_specs=[hbm...  170 us
    ppermute x16, waiting for transfers between devices, swap(): lax.ppermute(a, axis, [(k, k ^ bit) for k in range(mesh.shape[axis])])  108 us
    pallas_call x4, Pallas kernels, _grad_call(): pl.pallas_call(functools.partial(_grad_kernel, v0, 1.0 / tokens), grid_sp...  92.2 us
    pallas_call x3, Pallas kernels, _dw_call(): pl.pallas_call(functools.partial(_dw_kernel, steps), grid=(steps,), in_sp...  61 us
    ppermute x9, starting transfers between devices, z_shift(): return lax.ppermute(a, 'fsdp', [(k, (k + s) % n_z) for k in range(n_z)])  49.5 us
    ppermute x9, waiting for transfers between devices, z_shift(): return lax.ppermute(a, 'fsdp', [(k, (k + s) % n_z) for k in range(n_z)])  23.8 us
    pallas_call x1, Pallas kernels, _stats_call(): pl.pallas_call(_stats_kernel, in_specs=[vmem], out_specs=vmem, out_shape=...  14.1 us
    ppermute x16, starting transfers between devices, swap(): lax.ppermute(a, axis, [(k, k ^ bit) for k in range(mesh.shape[axis])])  13.4 us
  transfers between devices with their start and end apart: 25, of which 9 were waited for; matrix products, arithmetic and copies ran while one was open for 7% of the time, Pallas kernels for 22%

profile of v3, /device:TPU:0, one launch (start us, length us, event | category | flops | bytes accessed | tf_op | source)
XLA Modules:
  0.0 592.6 jit_solution(12214841265463356211)
XLA Ops:
  0.7 5.0 pad.4.w_ref
  5.6 169.6 %front.1 = (bf16[768,3200]{1,0:T(8,128)(2,1)}, s32[16,1,512]{2,1,0:T(1,128)}, f32[16,512,3200]{2,1,0:T(8,128)}, bf16[768,8192]{1,0:T(8,128)(2,1)}, f32[16,4,512]{2,1,0:T(4,128)}) custom-call(bf16[192,12800]{1,0:T(8,128)(2,1)} %pad.4.w_ref, bf16[512,768]{1,0:T(8,128)(2,1)} %x_ref.1, s32[1,512]{1,0:T(1,128)} %bitcast.99), custom_call_target="tpu_custom_call" | custom-call | tf_op jit(solution)/shard_map/front/pallas_call | solution.py:287
  176.1 14.1 %stats.1.st_ref = f32[16,4,512]{2,1,0:T(4,128)} custom-call(f32[16,4,512]{2,1,0:T(4,128)} %get-tuple-element.47.st_ref), custom_call_target="tpu_custom_call" | custom-call | tf_op jit(solution)/shard_map/stats/pallas_call | solution.py:361
  191.6 23.0 %grad_dx.4 = (bf16[16,512,1536]{2,1,0:T(8,128)(2,1)}, bf16[16,512,1664]{2,1,0:T(8,128)(2,1)}, f32[2,4,128,768]{3,2,1,0:T(8,128)}, f32[2,4,128,768]{3,2,1,0:T(8,128)}) custom-call(s32[2]{0:T(128)} %pad_add_fusion.ids_ref, f32[16,512,3200]{2,1,0:T(8,128)} %get-tuple-element.48.z_ref, bf16[768,3200]{1,0:T(8,128)(2,1)} %get-tuple-element.49.w_ref, ...), custom_call_target="tpu_custom_call" | custom-call | flops 10066329600 | bytes 39321600 | tf_op jit(solution)/shard_map/grad_dx/pallas_call | solution.py:390
  214.6 23.2 %grad_dx.5 = (bf16[16,512,1536]{2,1,0:T(8,128)(2,1)}, bf16[16,512,1664]{2,1,0:T(8,128)(2,1)}, f32[2,4,128,768]{3,2,1,0:T(8,128)}, f32[2,4,128,768]{3,2,1,0:T(8,128)}) custom-call(s32[2]{0:T(128)} %pad_add_fusion.ids_ref, f32[16,512,3200]{2,1,0:T(8,128)} %get-tuple-element.48.z_ref, ...), custom_call_target="tpu_custom_call", output_to_operand_aliasing={{0}: (5, {}), {1}: (6, {})} | custom-call | flops 10066329600 | bytes 39321600 | tf_op jit(solution)/shard_map/grad_dx/pallas_call | solution.py:390
  242.6 23.1 %grad_dx.6 = (bf16[16,512,1536]{2,1,0:T(8,128)(2,1)}, bf16[16,512,1664]{2,1,0:T(8,128)(2,1)}, f32[2,4,128,768]{3,2,1,0:T(8,128)}, f32[2,4,128,768]{3,2,1,0:T(8,128)}) custom-call(s32[2]{0:T(128)} %pad_add_fusion.ids_ref, f32[16,512,3200]{2,1,0:T(8,128)} %get-tuple-element.48.z_ref, ...), custom_call_target="tpu_custom_call", output_to_operand_aliasing={{0}: (5, {}), {1}: (6, {})} | custom-call | flops 10066329600 | bytes 39321600 | tf_op jit(solution)/shard_map/grad_dx/pallas_call | solution.py:390
  265.7 4.4 fusion.4
  270.1 22.9 %grad_dx.7 = (bf16[16,512,1536]{2,1,0:T(8,128)(2,1)}, bf16[16,512,1664]{2,1,0:T(8,128)(2,1)}, f32[2,4,128,768]{3,2,1,0:T(8,128)}, f32[2,4,128,768]{3,2,1,0:T(8,128)}) custom-call(s32[2]{0:T(128)} %pad_add_fusion.ids_ref, f32[16,512,3200]{2,1,0:T(8,128)} %get-tuple-element.48.z_ref, ...), custom_call_target="tpu_custom_call", output_to_operand_aliasing={{0}: (5, {}), {1}: (6, {})} | custom-call | flops 10066329600 | bytes 39321600 | tf_op jit(solution)/shard_map/grad_dx/pallas_call | solution.py:390
  295.3 4.4 fusion.2
  299.7 16.1 %dw.3 = bf16[768,768]{1,0:T(8,128)(2,1)} custom-call(bf16[768,8192]{1,0:T(8,128)(2,1)} %get-tuple-element.79.xt_ref, bf16[16,512,1536]{2,1,0:T(8,128)(2,1)} %get-tuple-element.72.g_ref), custom_call_target="tpu_custom_call" | custom-call | flops 9663676416 | bytes 25165824 | tf_op jit(solution)/shard_map/dw/pallas_call | solution.py:426
  315.8 14.4 %collective-permute-done.3 = f32[2,2,128,768]{3,2,1,0:T(8,128)} collective-permute-done((f32[2,2,128,768]{3,2,1,0:T(8,128)}, f32[2,2,128,768]{3,2,1,0:T(8,128)}, u32[]{:S(2)}, u32[]{:S(2)}) %collective-permute-start.3) | collective-permute-done | bytes 1572896 | tf_op jit(solution)/shard_map/ppermute | solution.py:486
  335.6 16.1 %dw.4 = bf16[768,768]{1,0:T(8,128)(2,1)} custom-call(bf16[768,8192]{1,0:T(8,128)(2,1)} %get-tuple-element.79.xt_ref, bf16[16,512,1536]{2,1,0:T(8,128)(2,1)} %get-tuple-element.72.g_ref), custom_call_target="tpu_custom_call" | custom-call | flops 9663676416 | bytes 25165824 | tf_op jit(solution)/shard_map/dw/pallas_call | solution.py:426
  362.7 7.7 %collective-permute-done.4 = f32[2,128,768]{2,1,0:T(8,128)} collective-permute-done((f32[2,128,768]{2,1,0:T(8,128)}, f32[2,128,768]{2,1,0:T(8,128)}, u32[]{:S(2)}, u32[]{:S(2)}) %collective-permute-start.4) | collective-permute-done | bytes 786464 | tf_op jit(solution)/shard_map/ppermute | solution.py:486
  372.6 28.7 %dw.5 = bf16[768,1664]{1,0:T(8,128)(2,1)} custom-call(bf16[768,8192]{1,0:T(8,128)(2,1)} %get-tuple-element.79.xt_ref, bf16[16,512,1664]{2,1,0:T(8,128)(2,1)} %get-tuple-element.80.g_ref), custom_call_target="tpu_custom_call" | custom-call | flops 20937965568 | bytes 39845888 | tf_op jit(solution)/shard_map/dw/pallas_call | solution.py:426
  408.5 12.5 %collective-permute-done.9 = f32[4,128,768]{2,1,0:T(8,128)} collective-permute-done((f32[4,128,768]{2,1,0:T(8,128)}, f32[4,128,768]{2,1,0:T(8,128)}, u32[]{:S(2)}, u32[]{:S(2)}) %collective-permute-start.9) | collective-permute-done | bytes 1572896 | tf_op jit(solution)/shard_map/ppermute | solution.py:486
  434.1 22.7 %collective-permute-done.11 = f32[2,128,768]{2,1,0:T(8,128)S(1)} collective-permute-done((f32[2,128,768]{2,1,0:T(8,128)}, f32[2,128,768]{2,1,0:T(8,128)S(1)}, u32[]{:S(2)}, u32[]{:S(2)}) %collective-permute-start.11) | collective-permute-done | bytes 786464 | tf_op jit(solution)/shard_map/ppermute | solution.py:486
  462.3 6.6 %collective-permute-done.17.refs_4_ = bf16[192,768]{1,0:T(8,128)(2,1)S(1)} collective-permute-done((bf16[192,768]{1,0:T(8,128)(2,1)}, bf16[192,768]{1,0:T(8,128)(2,1)S(1)}, u32[]{:S(2)}, u32[]{:S(2)}) %collective-permute-start.17) | collective-permute-done | bytes 294944 | tf_op jit(solution)/shard_map/ppermute | solution.py:483
  468.9 14.5 %collective-permute-start.16 = (bf16[192,768]{1,0:T(8,128)(2,1)S(1)}, bf16[192,768]{1,0:T(8,128)(2,1)S(1)}, u32[]{:S(2)}, u32[]{:S(2)}) collective-permute-start(bf16[192,768]{1,0:T(8,128)(2,1)S(1)} %copy-done.21), channel_id=1, source_target_pairs={{0,4},{4,8},{8,12},{12,0},{1,5},{5,9},{9,13},{13,1},{2,6},{6,10},{... | collective-permute-start | bytes 884744 | tf_op jit(solution)/shard_map/ppermute | solution.py:483
  483.5 13.5 %collective-permute-done.20.refs_7_ = bf16[192,768]{1,0:T(8,128)(2,1)S(1)} collective-permute-done((bf16[192,768]{1,0:T(8,128)(2,1)}, bf16[192,768]{1,0:T(8,128)(2,1)S(1)}, u32[]{:S(2)}, u32[]{:S(2)}) %collective-permute-start.20) | collective-permute-done | bytes 294944 | tf_op jit(solution)/shard_map/ppermute | solution.py:483
  497.0 18.8 %collective-permute-start.21 = (bf16[192,1664]{1,0:T(8,128)(2,1)S(1)}, bf16[192,1664]{1,0:T(8,128)(2,1)S(1)}, u32[]{:S(2)}, u32[]{:S(2)}) collective-permute-start(bf16[192,1664]{1,0:T(8,128)(2,1)S(1)} %copy-done.11), channel_id=1, source_target_pairs={{0,8},{4,12},{8,0},{12,4},{1,9},{5,13},{9,1},{13,5},{2,10},{6,14},... | collective-permute-start | bytes 1916936 | tf_op jit(solution)/shard_map/ppermute | solution.py:483
  515.8 3.5 collective-permute-start.24
  524.4 50.4 %collective-permute-done.15 = f32[128,768]{1,0:T(8,128)S(1)} collective-permute-done((f32[128,768]{1,0:T(8,128)S(1)}, f32[128,768]{1,0:T(8,128)S(1)}, u32[]{:S(2)}, u32[]{:S(2)}) %collective-permute-start.15) | collective-permute-done | bytes 393248 | tf_op jit(solution)/shard_map/ppermute | solution.py:486
  574.8 4.9 collective-permute-start.22
  586.5 5.0 place.1
  (115 shorter events, 64.5 us)
Async XLA Ops:
  214.6 23.8 %collective-permute-start = (f32[2,4,128,768]{3,2,1,0:T(8,128)}, f32[2,4,128,768]{3,2,1,0:T(8,128)}, u32[]{:S(2)}, u32[]{:S(2)}) collective-permute-start(f32[2,4,128,768]{3,2,1,0:T(8,128)} %get-tuple-element.57), channel_id=1, source_target_pairs={{0,1},{1,0},{2,3},{3,2},{4,5},{5,4},{6,7},{7,6},{8,9},{9,8},{10,11... | collective-permute-start | bytes 9437192 | tf_op jit(solution)/shard_map/ppermute | solution.py:486
  237.8 27.8 %collective-permute-start.1 = (f32[2,4,128,768]{3,2,1,0:T(8,128)}, f32[2,4,128,768]{3,2,1,0:T(8,128)}, u32[]{:S(2)}, u32[]{:S(2)}) collective-permute-start(f32[2,4,128,768]{3,2,1,0:T(8,128)} %get-tuple-element.64), channel_id=1, source_target_pairs={{0,1},{1,0},{2,3},{3,2},{4,5},{5,4},{6,7},{7,6},{8,9},{9,8},{10,11... | collective-permute-start | bytes 9437192 | tf_op jit(solution)/shard_map/ppermute | solution.py:486
  265.6 29.6 %collective-permute-start.2 = (f32[2,4,128,768]{3,2,1,0:T(8,128)}, f32[2,4,128,768]{3,2,1,0:T(8,128)}, u32[]{:S(2)}, u32[]{:S(2)}) collective-permute-start(f32[2,4,128,768]{3,2,1,0:T(8,128)} %get-tuple-element.70), channel_id=1, source_target_pairs={{0,1},{1,0},{2,3},{3,2},{4,5},{5,4},{6,7},{7,6},{8,9},{9,8},{10,11... | collective-permute-start | bytes 9437192 | tf_op jit(solution)/shard_map/ppermute | solution.py:486
  293.0 64.7 %collective-permute-start.5 = (f32[2,4,128,768]{3,2,1,0:T(8,128)}, f32[2,4,128,768]{3,2,1,0:T(8,128)}, u32[]{:S(2)}, u32[]{:S(2)}) collective-permute-start(f32[2,4,128,768]{3,2,1,0:T(8,128)} %get-tuple-element.77), channel_id=1, source_target_pairs={{0,1},{1,0},{2,3},{3,2},{4,5},{5,4},{6,7},{7,6},{8,9},{9,8},{10,11... | collective-permute-start | bytes 9437192 | tf_op jit(solution)/shard_map/ppermute | solution.py:486
  293.5 36.7 %collective-permute-start.3 = (f32[2,2,128,768]{3,2,1,0:T(8,128)}, f32[2,2,128,768]{3,2,1,0:T(8,128)}, u32[]{:S(2)}, u32[]{:S(2)}) collective-permute-start(f32[2,2,128,768]{3,2,1,0:T(8,128)} %get-tuple-element.97), channel_id=1, source_target_pairs={{0,4},{4,0},{8,12},{12,8},{1,5},{5,1},{9,13},{13,9},{2,6},{6,2},{1... | collective-permute-start | bytes 4718600 | tf_op jit(solution)/shard_map/ppermute | solution.py:486
  294.2 59.1 %collective-permute-start.6 = (f32[4,128,768]{2,1,0:T(8,128)}, f32[4,128,768]{2,1,0:T(8,128)}, u32[]{:S(2)}, u32[]{:S(2)}) collective-permute-start(f32[4,128,768]{2,1,0:T(8,128)} %get-tuple-element.95), channel_id=1, source_target_pairs={{0,2},{1,3},{2,0},{3,1},{4,6},{5,7},{6,4},{7,5},{8,10},{9,11},{10,... | collective-permute-start | bytes 4718600 | tf_op jit(solution)/shard_map/ppermute | solution.py:486
  333.6 36.8 %collective-permute-start.4 = (f32[2,128,768]{2,1,0:T(8,128)}, f32[2,128,768]{2,1,0:T(8,128)}, u32[]{:S(2)}, u32[]{:S(2)}) collective-permute-start(f32[2,128,768]{2,1,0:T(8,128)} %get-tuple-element.109), channel_id=1, source_target_pairs={{0,8},{4,12},{8,0},{12,4},{1,9},{5,13},{9,1},{13,5},{2,10},{6,14},... | collective-permute-start | bytes 2359304 | tf_op jit(solution)/shard_map/ppermute | solution.py:486
  351.7 52.8 %collective-permute-start.7 = (f32[4,128,768]{2,1,0:T(8,128)}, f32[4,128,768]{2,1,0:T(8,128)}, u32[]{:S(2)}, u32[]{:S(2)}) collective-permute-start(f32[4,128,768]{2,1,0:T(8,128)} %get-tuple-element.93), channel_id=1, source_target_pairs={{0,2},{1,3},{2,0},{3,1},{4,6},{5,7},{6,4},{7,5},{8,10},{9,11},{10,... | collective-permute-start | bytes 4718600 | tf_op jit(solution)/shard_map/ppermute | solution.py:486
  356.1 50.2 %collective-permute-start.8 = (f32[2,128,768]{2,1,0:T(8,128)}, f32[2,128,768]{2,1,0:T(8,128)}, u32[]{:S(2)}, u32[]{:S(2)}) collective-permute-start(f32[2,128,768]{2,1,0:T(8,128)} %get-tuple-element.107), channel_id=1, source_target_pairs={{0,4},{4,0},{8,12},{12,8},{1,5},{5,1},{9,13},{13,9},{2,6},{6,2},{1... | collective-permute-start | bytes 2359304 | tf_op jit(solution)/shard_map/ppermute | solution.py:486
  361.1 59.8 %collective-permute-start.9 = (f32[4,128,768]{2,1,0:T(8,128)}, f32[4,128,768]{2,1,0:T(8,128)}, u32[]{:S(2)}, u32[]{:S(2)}) collective-permute-start(f32[4,128,768]{2,1,0:T(8,128)} %get-tuple-element.91), channel_id=1, source_target_pairs={{0,2},{1,3},{2,0},{3,1},{4,6},{5,7},{6,4},{7,5},{8,10},{9,11},{10,... | collective-permute-start | bytes 4718600 | tf_op jit(solution)/shard_map/ppermute | solution.py:486
  406.3 22.0 %collective-permute-start.10 = (f32[2,128,768]{2,1,0:T(8,128)S(1)}, f32[2,128,768]{2,1,0:T(8,128)S(1)}, u32[]{:S(2)}, u32[]{:S(2)}) collective-permute-start(f32[2,128,768]{2,1,0:T(8,128)S(1)} %get-tuple-element.105), channel_id=1, source_target_pairs={{0,4},{4,0},{8,12},{12,8},{1,5},{5,1},{9,13},{13,9},{2,6},{6,2},{1... | collective-permute-start | bytes 2359304 | tf_op jit(solution)/shard_map/ppermute | solution.py:486
  423.6 33.1 %collective-permute-start.11 = (f32[2,128,768]{2,1,0:T(8,128)}, f32[2,128,768]{2,1,0:T(8,128)S(1)}, u32[]{:S(2)}, u32[]{:S(2)}) collective-permute-start(f32[2,128,768]{2,1,0:T(8,128)} %get-tuple-element.103), channel_id=1, source_target_pairs={{0,4},{4,0},{8,12},{12,8},{1,5},{5,1},{9,13},{13,9},{2,6},{6,2},{1... | collective-permute-start | bytes 2359304 | tf_op jit(solution)/shard_map/ppermute | solution.py:486
  426.0 33.0 %collective-permute-start.12 = (f32[128,768]{1,0:T(8,128)}, f32[128,768]{1,0:T(8,128)}, u32[]{:S(2)}, u32[]{:S(2)}) collective-permute-start(f32[128,768]{1,0:T(8,128)} %get-tuple-element.119), channel_id=1, source_target_pairs={{0,2},{1,3},{2,0},{3,1},{4,6},{5,7},{6,4},{7,5},{8,10},{9,11},{10,... | collective-permute-start | bytes 1179656 | tf_op jit(solution)/shard_map/ppermute | solution.py:486
  427.5 88.3 %collective-permute-start.13 = (f32[128,768]{1,0:T(8,128)S(1)}, f32[128,768]{1,0:T(8,128)}, u32[]{:S(2)}, u32[]{:S(2)}) collective-permute-start(f32[128,768]{1,0:T(8,128)S(1)} %get-tuple-element.125), channel_id=1, source_target_pairs={{0,8},{4,12},{8,0},{12,4},{1,9},{5,13},{9,1},{13,5},{2,10},{6,14},... | collective-permute-start | bytes 1179656 | tf_op jit(solution)/shard_map/ppermute | solution.py:486
  429.1 90.2 %collective-permute-start.14 = (f32[128,768]{1,0:T(8,128)}, f32[128,768]{1,0:T(8,128)}, u32[]{:S(2)}, u32[]{:S(2)}) collective-permute-start(f32[128,768]{1,0:T(8,128)} %get-tuple-element.123), channel_id=1, source_target_pairs={{0,8},{4,12},{8,0},{12,4},{1,9},{5,13},{9,1},{13,5},{2,10},{6,14},... | collective-permute-start | bytes 1179656 | tf_op jit(solution)/shard_map/ppermute | solution.py:486
  433.5 35.4 %collective-permute-start.17 = (bf16[192,768]{1,0:T(8,128)(2,1)}, bf16[192,768]{1,0:T(8,128)(2,1)S(1)}, u32[]{:S(2)}, u32[]{:S(2)}) collective-permute-start(bf16[192,768]{1,0:T(8,128)(2,1)} %get-tuple-element.113), channel_id=1, source_target_pairs={{0,4},{4,8},{8,12},{12,0},{1,5},{5,9},{9,13},{13,1},{2,6},{6,10},{... | collective-permute-start | bytes 884744 | tf_op jit(solution)/shard_map/ppermute | solution.py:483
  456.8 40.2 %collective-permute-start.20 = (bf16[192,768]{1,0:T(8,128)(2,1)}, bf16[192,768]{1,0:T(8,128)(2,1)S(1)}, u32[]{:S(2)}, u32[]{:S(2)}) collective-permute-start(bf16[192,768]{1,0:T(8,128)(2,1)} %get-tuple-element.112), channel_id=1, source_target_pairs={{0,8},{4,12},{8,0},{12,4},{1,9},{5,13},{9,1},{13,5},{2,10},{6,14},... | collective-permute-start | bytes 884744 | tf_op jit(solution)/shard_map/ppermute | solution.py:483
  459.0 38.0 %collective-permute-start.23 = (bf16[192,768]{1,0:T(8,128)(2,1)}, bf16[192,768]{1,0:T(8,128)(2,1)S(1)}, u32[]{:S(2)}, u32[]{:S(2)}) collective-permute-start(bf16[192,768]{1,0:T(8,128)(2,1)} %get-tuple-element.111), channel_id=1, source_target_pairs={{0,12},{4,0},{8,4},{12,8},{1,13},{5,1},{9,5},{13,9},{2,14},{6,2},{... | collective-permute-start | bytes 884744 | tf_op jit(solution)/shard_map/ppermute | solution.py:483
  468.9 52.5 %collective-permute-start.16 = (bf16[192,768]{1,0:T(8,128)(2,1)S(1)}, bf16[192,768]{1,0:T(8,128)(2,1)S(1)}, u32[]{:S(2)}, u32[]{:S(2)}) collective-permute-start(bf16[192,768]{1,0:T(8,128)(2,1)S(1)} %copy-done.21), channel_id=1, source_target_pairs={{0,4},{4,8},{8,12},{12,0},{1,5},{5,9},{9,13},{13,1},{2,6},{6,10},{... | collective-permute-start | bytes 884744 | tf_op jit(solution)/shard_map/ppermute | solution.py:483
  496.9 87.5 %collective-permute-start.18 = (bf16[192,1664]{1,0:T(8,128)(2,1)S(1)}, bf16[192,1664]{1,0:T(8,128)(2,1)S(1)}, u32[]{:S(2)}, u32[]{:S(2)}) collective-permute-start(bf16[192,1664]{1,0:T(8,128)(2,1)S(1)} %copy-done.12), channel_id=1, source_target_pairs={{0,4},{4,8},{8,12},{12,0},{1,5},{5,9},{9,13},{13,1},{2,6},{6,10},{... | collective-permute-start | bytes 1916936 | tf_op jit(solution)/shard_map/ppermute | solution.py:483
  497.0 87.5 %collective-permute-start.21 = (bf16[192,1664]{1,0:T(8,128)(2,1)S(1)}, bf16[192,1664]{1,0:T(8,128)(2,1)S(1)}, u32[]{:S(2)}, u32[]{:S(2)}) collective-permute-start(bf16[192,1664]{1,0:T(8,128)(2,1)S(1)} %copy-done.11), channel_id=1, source_target_pairs={{0,8},{4,12},{8,0},{12,4},{1,9},{5,13},{9,1},{13,5},{2,10},{6,14},... | collective-permute-start | bytes 1916936 | tf_op jit(solution)/shard_map/ppermute | solution.py:483
  515.8 68.7 %collective-permute-start.24 = (bf16[192,1664]{1,0:T(8,128)(2,1)S(1)}, bf16[192,1664]{1,0:T(8,128)(2,1)S(1)}, u32[]{:S(2)}, u32[]{:S(2)}) collective-permute-start(bf16[192,1664]{1,0:T(8,128)(2,1)S(1)} %copy-done.10), channel_id=1, source_target_pairs={{0,12},{4,0},{8,4},{12,8},{1,13},{5,1},{9,5},{13,9},{2,14},{6,2},{... | collective-permute-start | bytes 1916936 | tf_op jit(solution)/shard_map/ppermute | solution.py:483
  519.3 55.5 %collective-permute-start.15 = (f32[128,768]{1,0:T(8,128)S(1)}, f32[128,768]{1,0:T(8,128)S(1)}, u32[]{:S(2)}, u32[]{:S(2)}) collective-permute-start(f32[128,768]{1,0:T(8,128)S(1)} %get-tuple-element.121), channel_id=1, source_target_pairs={{0,8},{4,12},{8,0},{12,4},{1,9},{5,13},{9,1},{13,5},{2,10},{6,14},... | collective-permute-start | bytes 1179656 | tf_op jit(solution)/shard_map/ppermute | solution.py:486
  521.4 59.7 %collective-permute-start.19 = (bf16[192,768]{1,0:T(8,128)(2,1)S(1)}, bf16[192,768]{1,0:T(8,128)(2,1)S(1)}, u32[]{:S(2)}, u32[]{:S(2)}) collective-permute-start(bf16[192,768]{1,0:T(8,128)(2,1)S(1)} %copy-done.20), channel_id=1, source_target_pairs={{0,8},{4,12},{8,0},{12,4},{1,9},{5,13},{9,1},{13,5},{2,10},{6,14},... | collective-permute-start | bytes 884744 | tf_op jit(solution)/shard_map/ppermute | solution.py:483
  (23 other events, 595.5 us)
